TPU v7x, 1024 devices: a whole 4x4x32 slice. The times are simulated.
1024 devices in a mesh: dom: 64 (over y, z_lo, core), band: 16 (over x, z_hi).
Axes of the slice: x: 4, y: 4, z: 32 (z_hi: 4, z_lo: 8; z = z_hi * 8 + z_lo), core: 2. Of those that a mesh axis runs over, the one named last changes fastest.
Arguments:
- wavefunctions: bfloat16 [32768, 2048], P('dom', 'band'), may hold values from -6 to 6
- cell_ham: bfloat16 [128, 512, 512], P('dom'), may hold values from -0.25 to 0.25
- connectivity: int32 [128, 512], P('dom'), may hold values from 0 to 767, as said below
- inv_mass: float32 [32768], P('dom'), may hold values from 0.5 to 2
- cell_count: int32 [64], P('dom'), may hold values from 1 to 2, as said below
Outputs:
- filtered: bfloat16 [32768, 2048], P('dom', 'band')
- margin: float32 [2048, 2048], P('band', 'dom')
Inputs may be any that keep to these rules, and one draw needn't show every extreme that they name: `connectivity`: row c of domain d lists 512 indices into that domain's nodes extended by 128 nodes on each side; every extended index appears in some row of its domain. `cell_count`: some domain has all 2 cells live in every draw.
All inputs are finite; a program needn't handle non-finite values.
Results may differ from a plain program's by a relative error of at most 0.0052.
Values may be sent and summed in bfloat16 or wider, within the bound.
A program may use at most 32 MiB of HBM per device.

v0:
```python
import jax
import jax.numpy as jnp
from jax import lax
from jax.sharding import Mesh
from jax.sharding import PartitionSpec as P

DEGREE = 4
BAND = ("band_0", "band_1")


filter_center = 0.5
filter_halfwidth = 3.0


def padded(cells, sides, width):
    for axis, dim in sides:
        count = lax.axis_size(axis)
        head = lax.slice_in_dim(cells, 0, width, axis=dim)
        tail = lax.slice_in_dim(cells, cells.shape[dim] - width, cells.shape[dim], axis=dim)
        cells = jnp.concatenate(
            [
                lax.ppermute(tail, axis, [(i, (i + 1) % count) for i in range(count)]),
                cells,
                lax.ppermute(head, axis, [((i + 1) % count, i) for i in range(count)]),
            ],
            axis=dim,
        )
    return cells


def gathered_by_axis(shard, axes, dim):
    whole = shard
    for number in range(len(axes) - 1, -1, -1):
        whole = lax.all_gather(whole, axes[number], axis=dim, tiled=True)
    return whole


def split_up(shard, dim, count):
    shape = shard.shape
    tiles = shard.reshape(*shape[:dim], count, shape[dim] // count, *shape[dim + 1 :])
    return jnp.moveaxis(tiles, dim, 0)


def sent_and_summed(shard, axis, dim):
    count = lax.axis_size(axis)
    tiles = lax.all_to_all(split_up(shard, dim, count), axis, 0, 0, tiled=True)
    return jnp.sum(tiles, axis=0)


def apply_operator(current, cell_ham, connectivity, inv_mass, cell_count):
    owned = current.shape[0]
    width = current.shape[1]
    cells = cell_ham.shape[0]
    ghost = cell_ham.shape[1] // 4
    values = current.astype(jnp.bfloat16)
    extended = padded(values, (("dom", 0),), ghost)
    taken = extended[connectivity]
    prod = jnp.einsum("cij,cjb->cib", cell_ham, taken, preferred_element_type=jnp.float32)
    live = (lax.iota(jnp.int32, cells) < cell_count[0]).astype(jnp.float32)
    prod = prod * live[:, None, None]
    summed = jnp.zeros((owned + 2 * ghost, width), jnp.float32)
    summed = summed.at[connectivity.reshape(-1)].add(prod.reshape(-1, width))
    rims = jnp.concatenate([summed[:ghost], summed[ghost + owned :]], 0)
    returned = padded(rims, (("dom", 0),), ghost)
    middle = jnp.zeros((owned - 2 * ghost, width), jnp.float32)
    incoming = jnp.concatenate([returned[:ghost], middle, returned[3 * ghost :]], 0)
    return inv_mass[:, None] * (summed[ghost : ghost + owned] + incoming)


def tile_product(left, right):
    return lax.dot_general(
        left, right, (((0,), (0,)), ((), ())), preferred_element_type=jnp.float32
    )


def shards(wavefunctions, cell_ham, connectivity, inv_mass, cell_count):

    def operate(field):
        return apply_operator(field, cell_ham, connectivity, inv_mass, cell_count)

    previous = wavefunctions.astype(jnp.float32)
    current = (operate(previous) - filter_center * previous) / filter_halfwidth
    for step in range(DEGREE - 1):
        following = 2.0 * (operate(current) - filter_center * current) / filter_halfwidth - previous
        previous = current
        current = following
    filtered = current.astype(jnp.bfloat16)
    domains = lax.axis_size("dom")
    row_sums = tile_product(filtered, gathered_by_axis(filtered, BAND, 1))
    scale = 1.0 / jnp.sqrt(jnp.float32(filtered.shape[0] * domains))
    mine_cols = sent_and_summed(row_sums, "dom", 1)
    return (filtered, mine_cols * scale)


def solution(mesh):
    finer = Mesh(mesh.devices.reshape(mesh.shape["dom"], 4, 4), ("dom", "band_0", "band_1"))
    in_specs = (P("dom", BAND), P("dom", None, None), P("dom", None), P("dom"), P("dom"))
    out_specs = (P("dom", BAND), P(BAND, "dom"))
    return jax.shard_map(
        shards, mesh=finer, in_specs=in_specs, out_specs=out_specs, check_vma=False
    )
```

profile of v0, /device:TPU:1, one launch (start us, length us, event | category | flops | bytes accessed | tf_op | source)
XLA Modules:
  0.0 363.2 jit_solution(1423242756298160870)
XLA Ops:
  7.2 0.0 copy-start
  7.2 0.0 all-gather.2.cloned.1.call-start
  7.2 0.9 fusion.38
  8.1 4.9 %collective-permute-start = (bf16[128,128]{1,0:T(8,128)(2,1)S(1)}, bf16[128,128]{1,0:T(8,128)(2,1)S(1)}, u32[]{:S(2)}, u32[]{:S(2)}) collective-permute-start(bf16[128,128]{1,0:T(8,128)(2,1)S(1)} %get-tuple-element.22), channel_id=1, source_target_pairs={{0,16},{16,32},{32,48},{48,64},{64,80},{80,96},{96,112},{112,128},... | collective-permute-start | bytes 98312 | tf_op jit(solution)/shard_map/ppermute | solution.py:22
  13.0 13.0 %collective-permute-start.1 = (bf16[128,128]{1,0:T(8,128)(2,1)S(1)}, bf16[128,128]{1,0:T(8,128)(2,1)S(1)}, u32[]{:S(2)}, u32[]{:S(2)}) collective-permute-start(bf16[128,128]{1,0:T(8,128)(2,1)S(1)} %get-tuple-element.23), channel_id=1, source_target_pairs={{16,0},{32,16},{48,32},{64,48},{80,64},{96,80},{112,96},{128,112},... | collective-permute-start | bytes 98312 | tf_op jit(solution)/shard_map/ppermute | solution.py:24
  26.7 0.7 fusion.26
  27.4 0.7 copy.25
  28.1 0.9 pad_maximum_fusion
  29.1 3.2 gather_fusion
  32.3 0.0 copy-start.1
  32.3 0.0 copy-start.3
  32.3 0.5 fusion.3
  32.8 0.2 copy.12
  33.0 6.1 %scatter_custom_fusion = f32[768,128]{1,0:T(8,128)S(1)} fusion(s32[1024]{0:T(1024)S(1)} %bitcast.51, f32[1024,128]{1,0:T(8,128)S(1)} %bitcast.45, f32[]{:T(128)} %constant.8.clone.1), kind=kCustom, calls=%fused_computation.47 | custom fusion | flops 131072 | bytes 393220 | tf_op jit(solution)/shard_map/scatter-add | solution.py:62
  39.1 1.9 collective-permute-start.2
  41.1 12.4 %collective-permute-start.3 = (f32[128,128]{1,0:T(8,128)S(1)}, f32[128,128]{1,0:T(8,128)S(1)}, u32[]{:S(2)}, u32[]{:S(2)}) collective-permute-start(f32[128,128]{1,0:T(8,128)S(1)} %get-tuple-element.15), channel_id=1, source_target_pairs={{16,0},{32,16},{48,32},{64,48},{80,64},{96,80},{112,96},{128,112},... | collective-permute-start | bytes 196616 | tf_op jit(solution)/shard_map/ppermute | solution.py:24
  53.5 0.0 collective-permute-done.2
  53.5 0.8 collective-permute-done.3
  54.3 0.2 multiply_convert_fusion
  54.5 1.9 collective-permute-start.4
  56.5 13.4 %collective-permute-start.5 = (bf16[128,128]{1,0:T(8,128)(2,1)S(1)}, bf16[128,128]{1,0:T(8,128)(2,1)S(1)}, u32[]{:S(2)}, u32[]{:S(2)}) collective-permute-start(bf16[128,128]{1,0:T(8,128)(2,1)S(1)} %get-tuple-element.21), channel_id=1, source_target_pairs={{16,0},{32,16},{48,32},{64,48},{80,64},{96,80},{112,96},{128,112},... | collective-permute-start | bytes 98312 | tf_op jit(solution)/shard_map/ppermute | solution.py:24
  69.8 0.0 collective-permute-done.4
  69.8 0.8 collective-permute-done.5
  70.7 3.2 gather_fusion.1
  73.9 0.5 fusion.2
  74.4 0.2 copy.14
  74.6 6.1 %scatter_custom_fusion.1 = f32[768,128]{1,0:T(8,128)S(1)} fusion(s32[1024]{0:T(1024)S(1)} %bitcast.52, f32[1024,128]{1,0:T(8,128)S(1)} %bitcast.46, f32[]{:T(128)} %constant.8.clone.1), kind=kCustom, calls=%fused_computation.45 | custom fusion | flops 131072 | bytes 393220 | tf_op jit(solution)/shard_map/scatter-add | solution.py:62
  80.7 1.9 collective-permute-start.6
  82.7 13.2 %collective-permute-start.7 = (f32[128,128]{1,0:T(8,128)S(1)}, f32[128,128]{1,0:T(8,128)S(1)}, u32[]{:S(2)}, u32[]{:S(2)}) collective-permute-start(f32[128,128]{1,0:T(8,128)S(1)} %get-tuple-element.13), channel_id=1, source_target_pairs={{16,0},{32,16},{48,32},{64,48},{80,64},{96,80},{112,96},{128,112},... | collective-permute-start | bytes 196616 | tf_op jit(solution)/shard_map/ppermute | solution.py:24
  95.9 0.0 collective-permute-done.6
  95.9 0.9 collective-permute-done.7
  96.7 0.2 fusion.29
  97.0 1.9 collective-permute-start.8
  98.9 13.4 %collective-permute-start.9 = (bf16[128,128]{1,0:T(8,128)(2,1)S(1)}, bf16[128,128]{1,0:T(8,128)(2,1)S(1)}, u32[]{:S(2)}, u32[]{:S(2)}) collective-permute-start(bf16[128,128]{1,0:T(8,128)(2,1)S(1)} %get-tuple-element.19), channel_id=1, source_target_pairs={{16,0},{32,16},{48,32},{64,48},{80,64},{96,80},{112,96},{128,112},... | collective-permute-start | bytes 98312 | tf_op jit(solution)/shard_map/ppermute | solution.py:24
  112.3 0.0 collective-permute-done.8
  112.3 0.8 collective-permute-done.9
  113.1 3.2 gather_fusion.2
  116.4 0.5 fusion.1
  116.8 0.2 copy.16
  117.0 6.1 %scatter_custom_fusion.2 = f32[768,128]{1,0:T(8,128)S(1)} fusion(s32[1024]{0:T(1024)S(1)} %bitcast.53, f32[1024,128]{1,0:T(8,128)S(1)} %bitcast.47, f32[]{:T(128)} %constant.8.clone.1), kind=kCustom, calls=%fused_computation.43 | custom fusion | flops 131072 | bytes 393220 | tf_op jit(solution)/shard_map/scatter-add | solution.py:62
  123.2 1.9 collective-permute-start.10
  125.1 13.1 %collective-permute-start.11 = (f32[128,128]{1,0:T(8,128)S(1)}, f32[128,128]{1,0:T(8,128)S(1)}, u32[]{:S(2)}, u32[]{:S(2)}) collective-permute-start(f32[128,128]{1,0:T(8,128)S(1)} %get-tuple-element.11), channel_id=1, source_target_pairs={{16,0},{32,16},{48,32},{64,48},{80,64},{96,80},{112,96},{128,112},... | collective-permute-start | bytes 196616 | tf_op jit(solution)/shard_map/ppermute | solution.py:24
  138.3 0.0 collective-permute-done.10
  138.3 0.9 collective-permute-done.11
  139.1 0.2 fusion.27
  139.4 1.9 collective-permute-start.12
  141.3 13.4 %collective-permute-start.13 = (bf16[128,128]{1,0:T(8,128)(2,1)S(1)}, bf16[128,128]{1,0:T(8,128)(2,1)S(1)}, u32[]{:S(2)}, u32[]{:S(2)}) collective-permute-start(bf16[128,128]{1,0:T(8,128)(2,1)S(1)} %get-tuple-element.17), channel_id=1, source_target_pairs={{16,0},{32,16},{48,32},{64,48},{80,64},{96,80},{112,96},{128,112},... | collective-permute-start | bytes 98312 | tf_op jit(solution)/shard_map/ppermute | solution.py:24
  154.7 0.8 collective-permute-done.13
  155.5 3.2 gather_fusion.3
  158.8 0.5 fusion
  159.2 0.2 copy.18
  159.4 6.1 %scatter_custom_fusion.3 = f32[768,128]{1,0:T(8,128)S(1)} fusion(s32[1024]{0:T(1024)S(1)} %bitcast.54, f32[1024,128]{1,0:T(8,128)S(1)} %bitcast.44, f32[]{:T(128)} %constant.8.clone.1), kind=kCustom, calls=%fused_computation.41 | custom fusion | flops 131072 | bytes 393220 | tf_op jit(solution)/shard_map/scatter-add | solution.py:62
  165.6 1.9 collective-permute-start.14
  167.5 13.3 %collective-permute-start.15 = (f32[128,128]{1,0:T(8,128)S(1)}, f32[128,128]{1,0:T(8,128)S(1)}, u32[]{:S(2)}, u32[]{:S(2)}) collective-permute-start(f32[128,128]{1,0:T(8,128)S(1)} %get-tuple-element.9), channel_id=1, source_target_pairs={{16,0},{32,16},{48,32},{64,48},{80,64},{96,80},{112,96},{128,112},... | collective-permute-start | bytes 196616 | tf_op jit(solution)/shard_map/ppermute | solution.py:24
  180.9 0.9 collective-permute-done.15
  181.7 0.2 fusion.9
  181.9 0.0 copy-start.2
  182.0 58.4 %all_gather.6 = bf16[512,512]{1,0:T(8,128)(2,1)} all-gather(bf16[512,128]{1,0:T(8,128)(2,1)S(1)} %fusion.9), channel_id=1, replica_groups=mesh['dom'=64,'band_0'=4,'band_1'=4] {'band_1'}, dimensions={1}, use_global_device_ids=true | all-gather | bytes 655360 | tf_op jit(solution)/shard_map/all_gather | solution.py:34
  240.3 0.0 all-gather.2.cloned.1.call-update
  240.4 47.8 %all-gather.2.cloned.1.call-done = bf16[512,2048]{1,0:T(8,128)(2,1)} async-done(((bf16[512,512]{1,0:T(8,128)(2,1)}), bf16[512,2048]{1,0:T(8,128)(2,1)}) %all-gather.2.cloned.1.call-update) | async-done | bytes 2097168 | tf_op jit(solution)/shard_map/all_gather | solution.py:34
  288.2 2.5 fusion.39
  290.7 64.9 %all_to_all.5 = f32[64,128,32]{1,2,0:T(8,128)S(1)} all-to-all(f32[64,128,32]{1,2,0:T(8,128)S(1)} %bitcast.39), channel_id=1, replica_groups=mesh['dom'=64,'band_0'=4,'band_1'=4] {'dom'}, dimensions={0} | all-to-all | bytes 2097152 | tf_op jit(solution)/shard_map/all_to_all | solution.py:46
  355.7 0.1 reduce_sum.9
  355.8 0.6 broadcast_multiply_fusion
  (24 shorter events, 0.2 us)
Async XLA Ops:
  7.2 25.1 %copy-start = (bf16[2,512,512]{2,1,0:T(8,128)(2,1)S(1)}, bf16[2,512,512]{2,1,0:T(8,128)(2,1)}, u32[]{:S(2)}) copy-start(bf16[2,512,512]{2,1,0:T(8,128)(2,1)} %param.6) | copy-start | bytes 3145732
  7.2 281.0 %all-gather.2.cloned.1.call-start = ((), (), s32[]{:S(2)}) async-start(), calls=%async_computation.1 | async-start | bytes 2621440 | tf_op jit(solution)/shard_map/all_gather | solution.py:34
  8.1 20.0 %collective-permute-start = (bf16[128,128]{1,0:T(8,128)(2,1)S(1)}, bf16[128,128]{1,0:T(8,128)(2,1)S(1)}, u32[]{:S(2)}, u32[]{:S(2)}) collective-permute-start(bf16[128,128]{1,0:T(8,128)(2,1)S(1)} %get-tuple-element.22), channel_id=1, source_target_pairs={{0,16},{16,32},{32,48},{48,64},{64,80},{80,96},{96,112},{112,128},... | collective-permute-start | bytes 98312 | tf_op jit(solution)/shard_map/ppermute | solution.py:22
  13.0 15.1 %collective-permute-start.1 = (bf16[128,128]{1,0:T(8,128)(2,1)S(1)}, bf16[128,128]{1,0:T(8,128)(2,1)S(1)}, u32[]{:S(2)}, u32[]{:S(2)}) collective-permute-start(bf16[128,128]{1,0:T(8,128)(2,1)S(1)} %get-tuple-element.23), channel_id=1, source_target_pairs={{16,0},{32,16},{48,32},{64,48},{80,64},{96,80},{112,96},{128,112},... | collective-permute-start | bytes 98312 | tf_op jit(solution)/shard_map/ppermute | solution.py:24
  32.3 22.0 %copy-start.1 = (bf16[512,128]{1,0:T(8,128)(2,1)S(1)}, bf16[512,128]{1,0:T(8,128)(2,1)}, u32[]{:S(2)}) copy-start(bf16[512,128]{1,0:T(8,128)(2,1)} %param.5) | copy-start | bytes 393220
  32.3 22.0 %copy-start.3 = (f32[512]{0:T(512)S(1)}, f32[512]{0:T(512)}, u32[]{:S(2)}) copy-start(f32[512]{0:T(512)} %param.8) | copy-start | bytes 6148
  39.1 14.3 %collective-permute-start.2 = (f32[128,128]{1,0:T(8,128)S(1)}, f32[128,128]{1,0:T(8,128)S(1)}, u32[]{:S(2)}, u32[]{:S(2)}) collective-permute-start(f32[128,128]{1,0:T(8,128)S(1)} %get-tuple-element.14), channel_id=1, source_target_pairs={{0,16},{16,32},{32,48},{48,64},{64,80},{80,96},{96,112},{112,128},... | collective-permute-start | bytes 196616 | tf_op jit(solution)/shard_map/ppermute | solution.py:22
  41.1 13.2 %collective-permute-start.3 = (f32[128,128]{1,0:T(8,128)S(1)}, f32[128,128]{1,0:T(8,128)S(1)}, u32[]{:S(2)}, u32[]{:S(2)}) collective-permute-start(f32[128,128]{1,0:T(8,128)S(1)} %get-tuple-element.15), channel_id=1, source_target_pairs={{16,0},{32,16},{48,32},{64,48},{80,64},{96,80},{112,96},{128,112},... | collective-permute-start | bytes 196616 | tf_op jit(solution)/shard_map/ppermute | solution.py:24
  54.5 15.3 %collective-permute-start.4 = (bf16[128,128]{1,0:T(8,128)(2,1)S(1)}, bf16[128,128]{1,0:T(8,128)(2,1)S(1)}, u32[]{:S(2)}, u32[]{:S(2)}) collective-permute-start(bf16[128,128]{1,0:T(8,128)(2,1)S(1)} %get-tuple-element.20), channel_id=1, source_target_pairs={{0,16},{16,32},{32,48},{48,64},{64,80},{80,96},{96,112},{112,128},... | collective-permute-start | bytes 98312 | tf_op jit(solution)/shard_map/ppermute | solution.py:22
  56.5 14.2 %collective-permute-start.5 = (bf16[128,128]{1,0:T(8,128)(2,1)S(1)}, bf16[128,128]{1,0:T(8,128)(2,1)S(1)}, u32[]{:S(2)}, u32[]{:S(2)}) collective-permute-start(bf16[128,128]{1,0:T(8,128)(2,1)S(1)} %get-tuple-element.21), channel_id=1, source_target_pairs={{16,0},{32,16},{48,32},{64,48},{80,64},{96,80},{112,96},{128,112},... | collective-permute-start | bytes 98312 | tf_op jit(solution)/shard_map/ppermute | solution.py:24
  80.7 15.1 %collective-permute-start.6 = (f32[128,128]{1,0:T(8,128)S(1)}, f32[128,128]{1,0:T(8,128)S(1)}, u32[]{:S(2)}, u32[]{:S(2)}) collective-permute-start(f32[128,128]{1,0:T(8,128)S(1)} %get-tuple-element.12), channel_id=1, source_target_pairs={{0,16},{16,32},{32,48},{48,64},{64,80},{80,96},{96,112},{112,128},... | collective-permute-start | bytes 196616 | tf_op jit(solution)/shard_map/ppermute | solution.py:22
  82.7 14.1 %collective-permute-start.7 = (f32[128,128]{1,0:T(8,128)S(1)}, f32[128,128]{1,0:T(8,128)S(1)}, u32[]{:S(2)}, u32[]{:S(2)}) collective-permute-start(f32[128,128]{1,0:T(8,128)S(1)} %get-tuple-element.13), channel_id=1, source_target_pairs={{16,0},{32,16},{48,32},{64,48},{80,64},{96,80},{112,96},{128,112},... | collective-permute-start | bytes 196616 | tf_op jit(solution)/shard_map/ppermute | solution.py:24
  97.0 15.3 %collective-permute-start.8 = (bf16[128,128]{1,0:T(8,128)(2,1)S(1)}, bf16[128,128]{1,0:T(8,128)(2,1)S(1)}, u32[]{:S(2)}, u32[]{:S(2)}) collective-permute-start(bf16[128,128]{1,0:T(8,128)(2,1)S(1)} %get-tuple-element.18), channel_id=1, source_target_pairs={{0,16},{16,32},{32,48},{48,64},{64,80},{80,96},{96,112},{112,128},... | collective-permute-start | bytes 98312 | tf_op jit(solution)/shard_map/ppermute | solution.py:22
  98.9 14.2 %collective-permute-start.9 = (bf16[128,128]{1,0:T(8,128)(2,1)S(1)}, bf16[128,128]{1,0:T(8,128)(2,1)S(1)}, u32[]{:S(2)}, u32[]{:S(2)}) collective-permute-start(bf16[128,128]{1,0:T(8,128)(2,1)S(1)} %get-tuple-element.19), channel_id=1, source_target_pairs={{16,0},{32,16},{48,32},{64,48},{80,64},{96,80},{112,96},{128,112},... | collective-permute-start | bytes 98312 | tf_op jit(solution)/shard_map/ppermute | solution.py:24
  123.2 15.1 %collective-permute-start.10 = (f32[128,128]{1,0:T(8,128)S(1)}, f32[128,128]{1,0:T(8,128)S(1)}, u32[]{:S(2)}, u32[]{:S(2)}) collective-permute-start(f32[128,128]{1,0:T(8,128)S(1)} %get-tuple-element.10), channel_id=1, source_target_pairs={{0,16},{16,32},{32,48},{48,64},{64,80},{80,96},{96,112},{112,128},... | collective-permute-start | bytes 196616 | tf_op jit(solution)/shard_map/ppermute | solution.py:22
  125.1 14.0 %collective-permute-start.11 = (f32[128,128]{1,0:T(8,128)S(1)}, f32[128,128]{1,0:T(8,128)S(1)}, u32[]{:S(2)}, u32[]{:S(2)}) collective-permute-start(f32[128,128]{1,0:T(8,128)S(1)} %get-tuple-element.11), channel_id=1, source_target_pairs={{16,0},{32,16},{48,32},{64,48},{80,64},{96,80},{112,96},{128,112},... | collective-permute-start | bytes 196616 | tf_op jit(solution)/shard_map/ppermute | solution.py:24
  139.4 15.3 %collective-permute-start.12 = (bf16[128,128]{1,0:T(8,128)(2,1)S(1)}, bf16[128,128]{1,0:T(8,128)(2,1)S(1)}, u32[]{:S(2)}, u32[]{:S(2)}) collective-permute-start(bf16[128,128]{1,0:T(8,128)(2,1)S(1)} %get-tuple-element.16), channel_id=1, source_target_pairs={{0,16},{16,32},{32,48},{48,64},{64,80},{80,96},{96,112},{112,128},... | collective-permute-start | bytes 98312 | tf_op jit(solution)/shard_map/ppermute | solution.py:22
  141.3 14.2 %collective-permute-start.13 = (bf16[128,128]{1,0:T(8,128)(2,1)S(1)}, bf16[128,128]{1,0:T(8,128)(2,1)S(1)}, u32[]{:S(2)}, u32[]{:S(2)}) collective-permute-start(bf16[128,128]{1,0:T(8,128)(2,1)S(1)} %get-tuple-element.17), channel_id=1, source_target_pairs={{16,0},{32,16},{48,32},{64,48},{80,64},{96,80},{112,96},{128,112},... | collective-permute-start | bytes 98312 | tf_op jit(solution)/shard_map/ppermute | solution.py:24
  165.6 15.3 %collective-permute-start.14 = (f32[128,128]{1,0:T(8,128)S(1)}, f32[128,128]{1,0:T(8,128)S(1)}, u32[]{:S(2)}, u32[]{:S(2)}) collective-permute-start(f32[128,128]{1,0:T(8,128)S(1)} %get-tuple-element.8), channel_id=1, source_target_pairs={{0,16},{16,32},{32,48},{48,64},{64,80},{80,96},{96,112},{112,128},... | collective-permute-start | bytes 196616 | tf_op jit(solution)/shard_map/ppermute | solution.py:22
  167.5 14.2 %collective-permute-start.15 = (f32[128,128]{1,0:T(8,128)S(1)}, f32[128,128]{1,0:T(8,128)S(1)}, u32[]{:S(2)}, u32[]{:S(2)}) collective-permute-start(f32[128,128]{1,0:T(8,128)S(1)} %get-tuple-element.9), channel_id=1, source_target_pairs={{16,0},{32,16},{48,32},{64,48},{80,64},{96,80},{112,96},{128,112},... | collective-permute-start | bytes 196616 | tf_op jit(solution)/shard_map/ppermute | solution.py:24
  181.9 108.8 %copy-start.2 = (bf16[512,128]{1,0:T(8,128)(2,1)}, bf16[512,128]{1,0:T(8,128)(2,1)S(1)}, u32[]{:S(2)}) copy-start(bf16[512,128]{1,0:T(8,128)(2,1)S(1)} %fusion.9) | copy-start | bytes 393220
Sparse Core Ops, SparseCore 0:
  240.5 47.6 all-gather.1
where the time goes:
time: 364 us; the launch traced here: 363 us
  starting transfers between devices  124 us (34%)
  blocking collectives  123 us (34%)
  waiting for transfers between devices  53.8 us (15%)
  other arithmetic  27.7 us (8%)
  local copies, waits for them, and re-layouts  15.3 us (4%)
  between operations  15.2 us (4%)
  matrix products  4.45 us (1%)
    ppermute x8, starting transfers between devices, padded(): lax.ppermute(head, axis, [((i + 1) % count, i) for i in range(count)])  105 us
    all_to_all x1, blocking collectives, sent_and_summed(): tiles = lax.all_to_all(split_up(shard, dim, count), axis, 0, 0, tiled=True)  64.9 us
    all_gather x1, blocking collectives, gathered_by_axis(): whole = lax.all_gather(whole, axes[number], axis=dim, tiled=True)  58.4 us
    all_gather x1, waiting for transfers between devices, gathered_by_axis(): whole = lax.all_gather(whole, axes[number], axis=dim, tiled=True)  47.8 us
    scatter-add x4, other arithmetic, apply_operator(): summed = summed.at[connectivity.reshape(-1)].add(prod.reshape(-1, width))  24.5 us
    ppermute x8, starting transfers between devices, padded(): lax.ppermute(tail, axis, [(i, (i + 1) % count) for i in range(count)])  18.4 us
    gather x4, local copies, waits for them, and re-layouts, apply_operator(): taken = extended[connectivity]  12.8 us
  transfers between devices with their start and end apart: 17, of which 8 were waited for; matrix products, arithmetic and copies ran while one was open for 0% of the time, Pallas kernels for 0%

commit v1 on v0

v1 whole, which is shorter than its diff:
```python
import functools

import jax
import jax.numpy as jnp
from jax import lax
from jax.experimental import pallas as pl
from jax.experimental.pallas import tpu as pltpu
from jax.sharding import PartitionSpec as P

DEGREE = 4
CENTER = 0.5
HALFWIDTH = 3.0
NX, NY, NH, NZ = 4, 4, 4, 8
MESH = pl.DeviceIdType.MESH


def tile_of(size, most):
    return most if size % most == 0 else size


def kernel(
    shape, w_ref, h_ref, conn_ref, im_ref, cnt_ref, filt_ref, marg_ref,
    st, thi, tlo, ahi, alo, mext, imx, vext, ys, us_f, us, ur, rb, lb, pacc,
    es, er, zs, zr,
    s_w, r_w, s_im, r_im, s_u, r_u, s_r, r_r, s_l, r_l, s_e, r_e, s_z, r_z,
):
    nx, ny, nh, nz = shape
    own, width = w_ref.shape
    cells, npc, _ = h_ref.shape
    ghost = own // 4
    ext = own + 2 * ghost
    block = 2 * ghost
    hh = nh // 2
    out_rows = width // 4
    domains = ny * nz * 2

    d = lax.axis_index("dom")
    b = lax.axis_index("band")
    c = lax.rem(d, 2)
    zl = lax.rem(lax.div(d, 2), nz)
    y = lax.div(d, 2 * nz)
    zh = lax.rem(b, nh)
    x = lax.div(b, nh)

    def dev(xx, yy, hz, lz, core):
        return ((yy * nz + lz) * 2 + core, xx * nh + hz)

    def copy(src, dst, send, recv, where):
        return pltpu.make_async_remote_copy(
            src_ref=src, dst_ref=dst, send_sem=send, recv_sem=recv,
            device_id=where, device_id_type=MESH,
        )

    mine_l = lax.div(zh, hh) == c

    barrier = pltpu.get_barrier_semaphore()

    def greet(where):
        pl.semaphore_signal(barrier, inc=1, device_id=where, device_id_type=MESH)

    left = (lax.rem(d + domains - 1, domains), b)
    right = (lax.rem(d + 1, domains), b)
    greet(left)
    greet(right)
    for h in range(hh):
        for s in range(2):
            src_h = c * hh + h
            pl.when(jnp.logical_not((src_h == zh) & (c == s)))(
                functools.partial(greet, dev(x, y, src_h, zl, s)))
    for xx in range(nx):
        for s in range(2):
            pl.when(jnp.logical_not((x == xx) & (c == s)))(
                functools.partial(greet, dev(xx, y, zh, zl, s)))
    for yy in range(ny):
        pl.when(jnp.logical_not((x == y) & (y == yy)))(
            functools.partial(greet, dev(y, yy, zh, zl, c)))
    half = lax.div(zl, nz // 2)
    for lz in range(nz):
        pl.when(jnp.logical_not((zl == lz) & (c == half)))(
            functools.partial(greet, dev(x, y, zh, lz, half)))

    for cell in range(cells):
        live = cell < cnt_ref[0]
        cols = slice(cell * npc, (cell + 1) * npc)
        rt = tile_of(ext, 128)
        for r in range(ext // rt):
            ids = lax.broadcasted_iota(jnp.int32, (rt, npc), 0) + r * rt
            hit = (conn_ref[cell:cell + 1, :] == ids) & live
            st[r * rt:(r + 1) * rt, cols] = jnp.where(hit, 1.0, 0.0).astype(jnp.bfloat16)

    rt = tile_of(npc, 256)
    ct = tile_of(ext, 256)
    for cell in range(cells):
        def gather_cols(i, carry, cell=cell):
            r = pl.multiple_of(lax.div(i, ext // ct) * rt, rt)
            e = pl.multiple_of(lax.rem(i, ext // ct) * ct, ct)
            t = lax.dot_general(
                h_ref[cell, pl.ds(r, rt), :], st[pl.ds(e, ct), cell * npc:(cell + 1) * npc],
                (((1,), (1,)), ((), ())), preferred_element_type=jnp.float32)
            hi = t.astype(jnp.bfloat16)
            thi[pl.ds(cell * npc + r, rt), pl.ds(e, ct)] = hi
            tlo[pl.ds(cell * npc + r, rt), pl.ds(e, ct)] = (t - hi.astype(jnp.float32)).astype(jnp.bfloat16)
            return carry
        lax.fori_loop(0, (npc // rt) * (ext // ct), gather_cols, 0)

    art = tile_of(ext, 256)

    def scatter_rows(i, carry):
        r = pl.multiple_of(lax.div(i, ext // ct) * art, art)
        e = pl.multiple_of(lax.rem(i, ext // ct) * ct, ct)
        rows = st[pl.ds(r, art), :]
        a = jnp.dot(rows, thi[:, pl.ds(e, ct)], preferred_element_type=jnp.float32)
        a += jnp.dot(rows, tlo[:, pl.ds(e, ct)], preferred_element_type=jnp.float32)
        hi = a.astype(jnp.bfloat16)
        ahi[pl.ds(r, art), pl.ds(e, ct)] = hi
        alo[pl.ds(r, art), pl.ds(e, ct)] = (a - hi.astype(jnp.float32)).astype(jnp.bfloat16)
        return carry
    lax.fori_loop(0, (ext // art) * (ext // ct), scatter_rows, 0)

    def column(row):
        return jnp.transpose(jnp.broadcast_to(row, (row.shape[1], row.shape[1])))[:, :1]

    def spread(row):
        return jnp.broadcast_to(column(row), (ghost, width))

    for i in range(4):
        mext[ghost * (i + 1):ghost * (i + 2), :] = spread(im_ref[i:i + 1, :])
    vext[ghost:ghost + own, :] = w_ref[...]

    as_int = lambda flag: flag.astype(jnp.int32)
    total = (2 + (nh - as_int(mine_l)) + (2 * nx - 1) + (nx - as_int(x == y))
             + (nz - as_int(half == c)))
    pl.semaphore_wait(barrier, total)

    first = []
    for side, where in ((0, left), (1, right)):
        other = 1 - side
        rows = slice(0, ghost) if side == 0 else slice(own - ghost, own)
        land = slice(own + ghost, ext) if side == 0 else slice(0, ghost)
        first.append(copy(im_ref, imx.at[other], s_im.at[side], r_im.at[other], where))
        first.append(copy(w_ref.at[rows], vext.at[land], s_w.at[side], r_w.at[other], where))
    for one in first:
        one.start()
    for one in first:
        one.wait_recv()
    mext[0:ghost, :] = spread(imx[0, 3:4, :])
    mext[own + ghost:ext, :] = spread(imx[1, 0:1, :])
    ys[0] = vext[...].astype(jnp.float32)

    def side_of(which):
        return c if which == 0 else 1 - c

    def u_send(k, which):
        s = side_of(which)
        where = (lax.rem(d + domains + 2 * s - 1, domains), b)
        if k < DEGREE - 1:
            src, dst = us.at[k, s], ur.at[k, 1 - s]
        else:
            out = pl.ds(pl.multiple_of(s * ghost, ghost), ghost)
            src, dst = us.at[k, s, out], ur.at[k, 1 - s, out]
        return copy(src, dst, s_u.at[k, s], r_u.at[k, 1 - s], where)

    def u_recv(k, which):
        s = side_of(which)
        where = (lax.rem(d + domains + 2 * s - 1, domains), b)
        got = ur.at[k, s]
        if k == DEGREE - 1:
            got = ur.at[k, s, pl.ds(pl.multiple_of((1 - s) * ghost, ghost), ghost)]
        return copy(got, got, s_u.at[k, s], r_u.at[k, s], where)

    def product(rows):
        v = vext[...]
        return (jnp.dot(ahi[rows, :], v, preferred_element_type=jnp.float32)
                + jnp.dot(alo[rows, :], v, preferred_element_type=jnp.float32))

    def advance(k, rows, summed):
        cur, old = k % 2, 1 - k % 2
        av = mext[rows, :] * summed
        now = ys[cur, rows, :]
        if k == 0:
            new = (av - CENTER * now) * (1.0 / HALFWIDTH)
        else:
            new = (2.0 / HALFWIDTH) * (av - CENTER * now) - ys[old, rows, :]
        if k < DEGREE - 1:
            ys[old, rows, :] = new
        return new.astype(jnp.bfloat16)

    def place(own_row, n, value):
        rows = pl.ds(own_row, n)
        rb[x, c, rows, :] = value
        filt_ref[rows, :] = value

        @pl.when(mine_l)
        def _():
            lb[lax.rem(zh, hh), c, rows, :] = value

    piece = ((1, 3 * ghost), (3, ghost))

    def piece_rows(s, p):
        off = (1 - s) * ghost if p == 0 else s * 3 * ghost
        n = piece[p][1]
        if isinstance(off, int):
            return pl.ds(off, n)
        return pl.ds(pl.multiple_of(off, ghost), n)

    def r_send(xx, s, p):
        rows = piece_rows(c, p)
        ref = rb.at[x, c, rows]
        return copy(ref, ref, s_r.at[xx, s, p], r_r.at[x, c, p], dev(xx, y, zh, zl, s))

    def r_recv(xx, s, p):
        ref = rb.at[xx, s, piece_rows(s, p)]
        return copy(ref, ref, s_r.at[xx, s, p], r_r.at[xx, s, p], dev(xx, y, zh, zl, s))

    def l_send(hz, p):
        rows = piece_rows(c, p)
        return copy(rb.at[x, c, rows], lb.at[lax.rem(zh, hh), c, rows], s_l.at[hz, p],
                    r_l.at[lax.rem(zh, hh), c, p], dev(x, y, hz, zl, lax.div(zh, hh)))

    def l_recv(h, s, p):
        ref = lb.at[h, s, piece_rows(s, p)]
        return copy(ref, ref, s_l.at[h, p], r_l.at[h, s, p], dev(x, y, c * hh + h, zl, s))

    def not_self_r(xx, s):
        return jnp.logical_not((x == xx) & (c == s))

    def not_self_l(hz):
        return jnp.logical_not((zh == hz) & mine_l)

    def not_self_lr(h, s):
        return jnp.logical_not((zh == c * hh + h) & (c == s))

    def send_piece(p):
        for hz in range(nh):
            pl.when(not_self_l(hz))(lambda hz=hz: l_send(hz, p).start())
        for xx in range(nx):
            for s in range(2):
                pl.when(not_self_r(xx, s))(lambda xx=xx, s=s: r_send(xx, s, p).start())

    for k in range(DEGREE):
        last = k == DEGREE - 1
        offs = []
        for which in range(2):
            s = side_of(which)
            off = pl.multiple_of(s * own, block)
            offs.append((s, off))
            u = product(pl.ds(off, block))
            us_f[pl.ds(off, block), :] = u
            us[k, s] = u.astype(us.dtype)
            u_send(k, which).start()
        mid = slice(block, own)
        mid_new = advance(k, mid, product(mid))
        if last:
            place(ghost, own - block, mid_new)
        fresh = []
        for which in (1, 0):
            s, off = offs[which]
            u_recv(k, which).wait_recv()
            if not last:
                rows = pl.ds(off, block)
                fresh.append((rows, advance(
                    k, rows, us_f[rows, :] + ur[k, s].astype(jnp.float32))))
            else:
                inner = pl.multiple_of((1 - s) * ghost, ghost)
                rows = pl.ds(pl.multiple_of(off + inner, ghost), ghost)
                new = advance(
                    k, rows,
                    us_f[rows, :] + ur[k, s, pl.ds(inner, ghost), :].astype(jnp.float32))
                place(pl.multiple_of(s * 3 * ghost, ghost), ghost, new)
                send_piece(1 - which)
        if not last:
            vext[mid, :] = mid_new
            for rows, value in fresh:
                vext[rows, :] = value

    for p in range(2):
        for xx in range(nx):
            for s in range(2):
                pl.when(not_self_r(xx, s))(lambda xx=xx, s=s: r_recv(xx, s, p).wait_recv())
        for h in range(hh):
            for s in range(2):
                pl.when(not_self_lr(h, s))(lambda h=h, s=s: l_recv(h, s, p).wait_recv())
        for s in range(2):
            rows = piece_rows(s, p)
            right_op = jnp.concatenate([rb[xx, s, rows, :] for xx in range(nx)], axis=1)
            for h in range(hh):
                part = lax.dot_general(
                    lb[h, s, rows, :], right_op, (((0,), (0,)), ((), ())),
                    preferred_element_type=jnp.float32)
                hrows = slice(h * width, (h + 1) * width)
                if p == 0 and s == 0:
                    pacc[hrows, :] = part
                else:
                    pacc[hrows, :] += part

    def e_send(xx):
        return copy(es.at[xx], er.at[y], s_e.at[xx], r_e.at[y], dev(xx, x, zh, zl, c))

    def e_recv(yy):
        return copy(er.at[yy], er.at[yy], s_e.at[yy], r_e.at[yy], dev(y, yy, zh, zl, c))

    for xx in range(nx):
        value = pacc[:, xx * width:(xx + 1) * width].astype(es.dtype)
        away = jnp.logical_not((x == xx) & (x == y))

        @pl.when(away)
        def _(xx=xx, value=value):
            es[xx] = value
            e_send(xx).start()

        @pl.when(jnp.logical_not(away))
        def _(value=value):
            er[y] = value
    acc = None
    for yy in range(ny):
        pl.when(jnp.logical_not((x == y) & (y == yy)))(lambda yy=yy: e_recv(yy).wait_recv())
        term = er[yy].astype(jnp.float32)
        acc = term if acc is None else acc + term
    zs[...] = acc.astype(zs.dtype)

    targets = 2 * (nz // 2)

    def z_target(j):
        return c * (nz // 2) + j // 2, j % 2

    def z_away(j):
        lz, core = z_target(j)
        return jnp.logical_not((zl == lz) & (c == core))

    def z_send(j):
        lz, core = z_target(j)
        return copy(zs.at[j * out_rows:(j + 1) * out_rows], zr.at[zl], s_z.at[j], r_z.at[zl],
                    dev(x, y, zh, lz, core))

    def z_recv(lz):
        return copy(zr.at[lz], zr.at[lz], s_z.at[lz], r_z.at[lz], dev(x, y, zh, lz, half))

    for j in range(targets):
        pl.when(z_away(j))(lambda j=j: z_send(j).start())

        @pl.when(jnp.logical_not(z_away(j)))
        def _(j=j):
            zr[zl] = zs[j * out_rows:(j + 1) * out_rows, :]
    acc = None
    for lz in range(nz):
        pl.when(jnp.logical_not((zl == lz) & (c == half)))(lambda lz=lz: z_recv(lz).wait_recv())
        term = zr[lz].astype(jnp.float32)
        acc = term if acc is None else acc + term
    marg_ref[...] = acc * (1.0 / float(own * domains) ** 0.5)

    for one in first:
        one.wait_send()
    for k in range(DEGREE):
        for which in range(2):
            u_send(k, which).wait_send()
    for p in range(2):
        for hz in range(nh):
            pl.when(not_self_l(hz))(lambda hz=hz, p=p: l_send(hz, p).wait_send())
        for xx in range(nx):
            for s in range(2):
                pl.when(not_self_r(xx, s))(lambda xx=xx, s=s, p=p: r_send(xx, s, p).wait_send())
    for xx in range(nx):
        pl.when(jnp.logical_not((x == xx) & (x == y)))(lambda xx=xx: e_send(xx).wait_send())
    for j in range(targets):
        pl.when(z_away(j))(lambda j=j: z_send(j).wait_send())


def local(shape, wavefunctions, cell_ham, connectivity, inv_mass, cell_count):
    nx, ny, nh, nz = shape
    own, width = wavefunctions.shape
    cells, npc, _ = cell_ham.shape
    ghost = own // 4
    ext = own + 2 * ghost
    block = 2 * ghost
    hh = nh // 2
    out_rows = width // 4
    bf, f32 = jnp.bfloat16, jnp.float32
    sent = f32
    dma = pltpu.SemaphoreType.DMA
    vm = pl.BlockSpec(memory_space=pltpu.VMEM)
    filtered, rows = pl.pallas_call(
        functools.partial(kernel, shape),
        out_shape=(jax.ShapeDtypeStruct((own, width), bf), jax.ShapeDtypeStruct((out_rows, width), f32)),
        in_specs=[vm, vm, vm, vm, pl.BlockSpec(memory_space=pltpu.SMEM)],
        out_specs=(vm, vm),
        scratch_shapes=[
            pltpu.VMEM((ext, cells * npc), bf),
            pltpu.VMEM((cells * npc, ext), bf),
            pltpu.VMEM((cells * npc, ext), bf),
            pltpu.VMEM((ext, ext), bf),
            pltpu.VMEM((ext, ext), bf),
            pltpu.VMEM((ext, width), f32),
            pltpu.VMEM((2, 4, ghost), f32),
            pltpu.VMEM((ext, width), bf),
            pltpu.VMEM((2, ext, width), f32),
            pltpu.VMEM((ext, width), f32),
            pltpu.VMEM((DEGREE, 2, block, width), sent),
            pltpu.VMEM((DEGREE, 2, block, width), sent),
            pltpu.VMEM((nx, 2, own, width), bf),
            pltpu.VMEM((hh, 2, own, width), bf),
            pltpu.VMEM((hh * width, nx * width), f32),
            pltpu.VMEM((nx, hh * width, width), bf),
            pltpu.VMEM((ny, hh * width, width), bf),
            pltpu.VMEM((hh * width, width), bf),
            pltpu.VMEM((nz, out_rows, width), bf),
            dma((2,)), dma((2,)), dma((2,)), dma((2,)),
            dma((DEGREE, 2)), dma((DEGREE, 2)),
            dma((nx, 2, 2)), dma((nx, 2, 2)),
            dma((nh, 2)), dma((hh, 2, 2)),
            dma((nx,)), dma((ny,)),
            dma((nz,)), dma((nz,)),
        ],
        compiler_params=pltpu.CompilerParams(
            collective_id=0, has_side_effects=True, vmem_limit_bytes=48 * 1024 * 1024),
        name="filter_margin",
    )(wavefunctions, cell_ham, connectivity, inv_mass.reshape(4, ghost), cell_count)
    return filtered, rows.T


def solution(mesh, shape=(NX, NY, NH, NZ)):
    return jax.shard_map(
        functools.partial(local, shape), mesh=mesh,
        in_specs=(P("dom", "band"), P("dom", None, None), P("dom", None), P("dom"), P("dom")),
        out_specs=(P("dom", "band"), P("band", "dom")),
        check_vma=False,
    )
```

time: 364 us -> 125 us (0.34)
  starting transfers between devices: 124 us -> 0 us
  blocking collectives: 123 us -> 0 us
  Pallas kernels: 0 us -> 118 us
  waiting for transfers between devices: 53.8 us -> 0 us
  other arithmetic: 27.7 us -> 0 us
  between operations: 15.2 us -> 1.31 us
  local copies, waits for them, and re-layouts: 15.3 us -> 4.09 us
  matrix products: 4.45 us -> 0 us
    ppermute x16 -> x0, starting transfers between devices: 123 us -> none  [the longest x8 105 us: padded(): lax.ppermute(head, axis, [((i + 1) % count, i) for i in range(count)])]
    pallas_call x0 -> x1, Pallas kernels: none -> 118 us  [local(): pl.pallas_call(functools.partial(kernel, shape), out_shape=(jax.ShapeDtyp...]
    all_to_all x1 -> x0, blocking collectives: 64.9 us -> none  [sent_and_summed(): tiles = lax.all_to_all(split_up(shard, dim, count), axis, 0, 0, tiled=True)]
    all_gather x1 -> x0, blocking collectives: 58.4 us -> none  [gathered_by_axis(): whole = lax.all_gather(whole, axes[number], axis=dim, tiled=True)]
    all_gather x1 -> x0, waiting for transfers between devices: 47.8 us -> none  [gathered_by_axis(): whole = lax.all_gather(whole, axes[number], axis=dim, tiled=True)]
    scatter-add x4 -> x0, other arithmetic: 24.5 us -> none  [apply_operator(): summed = summed.at[connectivity.reshape(-1)].add(prod.reshape(-1, width))]
    gather x4 -> x0, local copies, waits for them, and re-layouts: 12.8 us -> none  [apply_operator(): taken = extended[connectivity]]
    ppermute x16 -> x0, waiting for transfers between devices: 5.96 us -> none  [the longest x8 5.94 us: padded(): lax.ppermute(head, axis, [((i + 1) % count, i) for i in range(count)])]
  transfers between devices with their start and end apart: 17 -> 0, of which waited for: 8 -> 0; matrix products, arithmetic and copies ran while one was open for 0% -> 0% of each run, Pallas kernels for 0% -> 0%
where the time goes in v1:
time: 125 us; the launch traced here: 124 us
  Pallas kernels  118 us (94%)
  local copies, waits for them, and re-layouts  4.09 us (3%)
  between operations  1.31 us (1%)
    pallas_call x1, Pallas kernels, local(): pl.pallas_call(functools.partial(kernel, shape), out_shape=(jax.ShapeDtyp...  118 us
    unnamed x10, local copies, waits for them, and re-layouts  4.09 us

profile of v1, /device:TPU:1, one launch (start us, length us, event | category | flops | bytes accessed | tf_op | source)
XLA Modules:
  0.0 123.9 jit_solution(8155265607761838652)
XLA Ops:
  0.6 0.0 copy-start.3
  1.3 0.0 copy-done.3
  1.3 0.0 copy-start
  1.3 1.2 copy-done
  2.5 0.0 copy-start.1
  2.5 0.9 copy-done.1
  3.4 0.0 copy-start.2
  3.4 0.7 copy-done.2
  4.1 118.5 %filter_margin.1 = (bf16[512,128]{1,0:T(8,128)(2,1)S(1)}, f32[32,128]{1,0:T(8,128)S(1)}) custom-call(bf16[512,128]{1,0:T(8,128)(2,1)S(1)} %copy-done.1, bf16[2,512,512]{2,1,0:T(8,128)(2,1)S(1)} %copy-done, s32[2,512]{1,0:T(2,128)S(1)} %copy-done.2, f32[4,128]{1,0:T(4,128)S(1)} %bitcast.3, s32[1]{0:T(128)S(6)} %copy.9.cnt_ref), custom_call_target="tpu_custom_call" | custom-call | tf_op jit(solution)/shard_map/filter_margin/pallas_call | solution.py:381
  122.6 0.7 copy.10
  123.3 0.6 copy.11
Async XLA Ops:
  0.6 0.7 copy-start.3
  1.3 1.2 copy-start
  2.5 0.9 copy-start.1
  3.4 0.7 copy-start.2

commit v2 on v1

--- a/solution.py
+++ b/solution.py
@@ -20,9 +20,9 @@
 
 def kernel(
     shape, w_ref, h_ref, conn_ref, im_ref, cnt_ref, filt_ref, marg_ref,
-    st, thi, tlo, ahi, alo, mext, imx, vext, ys, us_f, us, ur, rb, lb, pacc,
+    st, thi, tlo, ahi, alo, mext, imx, vext, ys, us_f, us, ur, rb, lb, pacc, px,
     es, er, zs, zr,
-    s_w, r_w, s_im, r_im, s_u, r_u, s_r, r_r, s_l, r_l, s_e, r_e, s_z, r_z,
+    s_w, r_w, s_im, r_im, s_u, r_u, s_r, r_r, s_l, r_l, s_p, r_p, s_e, r_e, s_z, r_z,
 ):
     nx, ny, nh, nz = shape
     own, width = w_ref.shape
@@ -51,7 +51,16 @@
             device_id=where, device_id_type=MESH,
         )
 
-    mine_l = lax.div(zh, hh) == c
+    ring = {"h": (zh, nh), "x": (x, nx)}
+
+    def at(axis, step):
+        place, count = ring[axis]
+        return lax.rem(place + count + step, count)
+
+    def beside(axis, step):
+        if axis == "h":
+            return dev(x, y, at("h", step), zl, c)
+        return dev(at("x", step), y, zh, zl, c)
 
     barrier = pltpu.get_barrier_semaphore()
 
@@ -62,15 +71,13 @@
     right = (lax.rem(d + 1, domains), b)
     greet(left)
     greet(right)
-    for h in range(hh):
-        for s in range(2):
-            src_h = c * hh + h
-            pl.when(jnp.logical_not((src_h == zh) & (c == s)))(
-                functools.partial(greet, dev(x, y, src_h, zl, s)))
-    for xx in range(nx):
-        for s in range(2):
-            pl.when(jnp.logical_not((x == xx) & (c == s)))(
-                functools.partial(greet, dev(xx, y, zh, zl, s)))
+    greet(beside("h", 1))
+    greet(beside("h", -1))
+    if nx > 1:
+        greet(beside("x", 1))
+        greet(beside("x", -1))
+    partner = dev(x, y, zh, zl, 1 - c)
+    greet(partner)
     for yy in range(ny):
         pl.when(jnp.logical_not((x == y) & (y == yy)))(
             functools.partial(greet, dev(y, yy, zh, zl, c)))
@@ -128,7 +135,7 @@
     vext[ghost:ghost + own, :] = w_ref[...]
 
     as_int = lambda flag: flag.astype(jnp.int32)
-    total = (2 + (nh - as_int(mine_l)) + (2 * nx - 1) + (nx - as_int(x == y))
+    total = (2 + 2 + (2 if nx > 1 else 0) + 1 + (nx - as_int(x == y))
              + (nz - as_int(half == c)))
     pl.semaphore_wait(barrier, total)
 
@@ -187,55 +194,43 @@
 
     def place(own_row, n, value):
         rows = pl.ds(own_row, n)
-        rb[x, c, rows, :] = value
+        lb[zh, rows, :] = value
+        rb[x, rows, :] = value
         filt_ref[rows, :] = value
 
-        @pl.when(mine_l)
-        def _():
-            lb[lax.rem(zh, hh), c, rows, :] = value
-
-    piece = ((1, 3 * ghost), (3, ghost))
-
-    def piece_rows(s, p):
-        off = (1 - s) * ghost if p == 0 else s * 3 * ghost
-        n = piece[p][1]
-        if isinstance(off, int):
-            return pl.ds(off, n)
-        return pl.ds(pl.multiple_of(off, ghost), n)
-
-    def r_send(xx, s, p):
-        rows = piece_rows(c, p)
-        ref = rb.at[x, c, rows]
-        return copy(ref, ref, s_r.at[xx, s, p], r_r.at[x, c, p], dev(xx, y, zh, zl, s))
-
-    def r_recv(xx, s, p):
-        ref = rb.at[xx, s, piece_rows(s, p)]
-        return copy(ref, ref, s_r.at[xx, s, p], r_r.at[xx, s, p], dev(xx, y, zh, zl, s))
-
-    def l_send(hz, p):
-        rows = piece_rows(c, p)
-        return copy(rb.at[x, c, rows], lb.at[lax.rem(zh, hh), c, rows], s_l.at[hz, p],
-                    r_l.at[lax.rem(zh, hh), c, p], dev(x, y, hz, zl, lax.div(zh, hh)))
-
-    def l_recv(h, s, p):
-        ref = lb.at[h, s, piece_rows(s, p)]
-        return copy(ref, ref, s_l.at[h, p], r_l.at[h, s, p], dev(x, y, c * hh + h, zl, s))
-
-    def not_self_r(xx, s):
-        return jnp.logical_not((x == xx) & (c == s))
-
-    def not_self_l(hz):
-        return jnp.logical_not((zh == hz) & mine_l)
-
-    def not_self_lr(h, s):
-        return jnp.logical_not((zh == c * hh + h) & (c == s))
+    def piece_rows(core, p):
+        if p == 0:
+            return pl.ds(pl.multiple_of((1 - core) * ghost, ghost), 3 * ghost)
+        return pl.ds(pl.multiple_of(core * 3 * ghost, ghost), ghost)
+
+    bufs = {"h": (lb, s_l, r_l), "x": (rb, s_r, r_r)}
+    toward = 2 * c - 1
+
+    def block_send(axis, i, p):
+        buf, send, recv = bufs[axis]
+        step = (1, -1, -toward)[i]
+        slot = ring[axis][0] if i < 2 else at(axis, toward)
+        ref = buf.at[slot, piece_rows(c, p)]
+        return copy(ref, ref, send.at[i, p], recv.at[i, p], beside(axis, step))
+
+    def block_recv(axis, i, p):
+        buf, send, recv = bufs[axis]
+        slot = at(axis, (-1, 1, 2)[i])
+        step = (-1, 1, toward)[i]
+        ref = buf.at[slot, piece_rows(c, p)]
+        return copy(ref, ref, send.at[i, p], recv.at[i, p], beside(axis, step))
+
+    axes = ("h", "x") if nx > 1 else ("h",)
 
     def send_piece(p):
-        for hz in range(nh):
-            pl.when(not_self_l(hz))(lambda hz=hz: l_send(hz, p).start())
-        for xx in range(nx):
-            for s in range(2):
-                pl.when(not_self_r(xx, s))(lambda xx=xx, s=s: r_send(xx, s, p).start())
+        for axis in axes:
+            for i in range(2):
+                block_send(axis, i, p).start()
+
+    def pass_on(axis, p):
+        for i in range(2):
+            block_recv(axis, i, p).wait_recv()
+        block_send(axis, 2, p).start()
 
     for k in range(DEGREE):
         last = k == DEGREE - 1
@@ -274,24 +269,33 @@
                 vext[rows, :] = value
 
     for p in range(2):
-        for xx in range(nx):
-            for s in range(2):
-                pl.when(not_self_r(xx, s))(lambda xx=xx, s=s: r_recv(xx, s, p).wait_recv())
-        for h in range(hh):
-            for s in range(2):
-                pl.when(not_self_lr(h, s))(lambda h=h, s=s: l_recv(h, s, p).wait_recv())
-        for s in range(2):
-            rows = piece_rows(s, p)
-            right_op = jnp.concatenate([rb[xx, s, rows, :] for xx in range(nx)], axis=1)
-            for h in range(hh):
-                part = lax.dot_general(
-                    lb[h, s, rows, :], right_op, (((0,), (0,)), ((), ())),
-                    preferred_element_type=jnp.float32)
-                hrows = slice(h * width, (h + 1) * width)
-                if p == 0 and s == 0:
-                    pacc[hrows, :] = part
-                else:
-                    pacc[hrows, :] += part
+        for axis in reversed(axes):
+            pass_on(axis, p)
+    if nx > 1:
+        for p in range(2):
+            block_recv("x", 2, p).wait_recv()
+    right_op = jnp.concatenate([rb[xx] for xx in range(nx)], axis=1)
+
+    def p_rows(o):
+        return pl.ds(pl.multiple_of(o * width, width), width)
+
+    def p_send(o):
+        h = lax.rem(o, hh)
+        return copy(pacc.at[p_rows(o)], px.at[h], s_p.at[h], r_p.at[h], partner)
+
+    def p_recv(h):
+        return copy(px.at[h], px.at[h], s_p.at[h], r_p.at[h], partner)
+
+    for step in (0, -1, 1, 2):
+        o = at("h", step)
+        if step == 2:
+            for p in range(2):
+                block_recv("h", 2, p).wait_recv()
+        pacc[p_rows(o), :] = lax.dot_general(
+            lb[o], right_op, (((0,), (0,)), ((), ())), preferred_element_type=jnp.float32)
+        pl.when(lax.div(o, hh) != c)(lambda o=o: p_send(o).start())
+    for h in range(hh):
+        p_recv(h).wait_recv()
 
     def e_send(xx):
         return copy(es.at[xx], er.at[y], s_e.at[xx], r_e.at[y], dev(xx, x, zh, zl, c))
@@ -299,8 +303,10 @@
     def e_recv(yy):
         return copy(er.at[yy], er.at[yy], s_e.at[yy], r_e.at[yy], dev(y, yy, zh, zl, c))
 
+    sums = [pacc[p_rows(c * hh + h), :] + px[h] for h in range(hh)]
     for xx in range(nx):
-        value = pacc[:, xx * width:(xx + 1) * width].astype(es.dtype)
+        cols = slice(xx * width, (xx + 1) * width)
+        value = jnp.concatenate([one[:, cols] for one in sums], axis=0).astype(es.dtype)
         away = jnp.logical_not((x == xx) & (x == y))
 
         @pl.when(away)
@@ -354,11 +360,11 @@
         for which in range(2):
             u_send(k, which).wait_send()
     for p in range(2):
-        for hz in range(nh):
-            pl.when(not_self_l(hz))(lambda hz=hz, p=p: l_send(hz, p).wait_send())
-        for xx in range(nx):
-            for s in range(2):
-                pl.when(not_self_r(xx, s))(lambda xx=xx, s=s, p=p: r_send(xx, s, p).wait_send())
+        for axis in axes:
+            for i in range(3):
+                block_send(axis, i, p).wait_send()
+    for h in range(hh):
+        p_send((1 - c) * hh + h).wait_send()
     for xx in range(nx):
         pl.when(jnp.logical_not((x == xx) & (x == y)))(lambda xx=xx: e_send(xx).wait_send())
     for j in range(targets):
@@ -396,17 +402,18 @@
             pltpu.VMEM((ext, width), f32),
             pltpu.VMEM((DEGREE, 2, block, width), sent),
             pltpu.VMEM((DEGREE, 2, block, width), sent),
-            pltpu.VMEM((nx, 2, own, width), bf),
-            pltpu.VMEM((hh, 2, own, width), bf),
-            pltpu.VMEM((hh * width, nx * width), f32),
+            pltpu.VMEM((nx, own, width), bf),
+            pltpu.VMEM((nh, own, width), bf),
+            pltpu.VMEM((nh * width, nx * width), f32),
+            pltpu.VMEM((hh, width, nx * width), f32),
             pltpu.VMEM((nx, hh * width, width), bf),
             pltpu.VMEM((ny, hh * width, width), bf),
             pltpu.VMEM((hh * width, width), bf),
             pltpu.VMEM((nz, out_rows, width), bf),
             dma((2,)), dma((2,)), dma((2,)), dma((2,)),
             dma((DEGREE, 2)), dma((DEGREE, 2)),
-            dma((nx, 2, 2)), dma((nx, 2, 2)),
-            dma((nh, 2)), dma((hh, 2, 2)),
+            dma((3, 2)), dma((3, 2)), dma((3, 2)), dma((3, 2)),
+            dma((hh,)), dma((hh,)),
             dma((nx,)), dma((ny,)),
             dma((nz,)), dma((nz,)),
         ],

time: 125 us -> 117 us (0.936)
  the two profiles are of different devices: /device:TPU:1 before, /device:TPU:17 now
where the time goes in v2:
time: 117 us
  Pallas kernels  112 us (96%)
  local copies, waits for them, and re-layouts  4.09 us (3%)
  between operations  1.31 us (1%)
    pallas_call x1, Pallas kernels, local(): pl.pallas_call(functools.partial(kernel, shape), out_shape=(jax.ShapeDtyp...  112 us
    unnamed x10, local copies, waits for them, and re-layouts  4.09 us

profile of v2, /device:TPU:17, one launch (start us, length us, event | category | flops | bytes accessed | tf_op | source)
XLA Modules:
  0.0 117.2 jit_solution(14199094437025619444)
XLA Ops:
  0.6 0.0 copy-start.3
  1.3 0.0 copy-done.3
  1.3 0.0 copy-start
  1.3 1.2 %copy-done = bf16[2,512,512]{2,1,0:T(8,128)(2,1)S(1)} copy-done((bf16[2,512,512]{2,1,0:T(8,128)(2,1)S(1)}, bf16[2,512,512]{2,1,0:T(8,128)(2,1)}, u32[]{:S(2)}) %copy-start) | copy-done | bytes 1048600
  2.5 0.0 copy-start.1
  2.5 0.9 copy-done.1
  3.4 0.0 copy-start.2
  3.4 0.7 copy-done.2
  4.1 111.8 %filter_margin.1 = (bf16[512,128]{1,0:T(8,128)(2,1)S(1)}, f32[32,128]{1,0:T(8,128)S(1)}) custom-call(bf16[512,128]{1,0:T(8,128)(2,1)S(1)} %copy-done.1, bf16[2,512,512]{2,1,0:T(8,128)(2,1)S(1)} %copy-done, s32[2,512]{1,0:T(2,128)S(1)} %copy-done.2, f32[4,128]{1,0:T(4,128)S(1)} %bitcast.3, s32[1]{0:T(128)S(6)} %copy.9.cnt_ref), custom_call_target="tpu_custom_call" | custom-call | tf_op jit(solution)/shard_map/filter_margin/pallas_call | solution.py:387
  115.9 0.7 copy.10
  116.6 0.6 copy.11
Async XLA Ops:
  0.6 0.7 copy-start.3
  1.3 1.2 %copy-start = (bf16[2,512,512]{2,1,0:T(8,128)(2,1)S(1)}, bf16[2,512,512]{2,1,0:T(8,128)(2,1)}, u32[]{:S(2)}) copy-start(bf16[2,512,512]{2,1,0:T(8,128)(2,1)} %h_ref.1) | copy-start | bytes 3145732
  2.5 0.9 copy-start.1
  3.4 0.7 copy-start.2

commit v3 on v2

--- a/solution.py
+++ b/solution.py
@@ -19,18 +19,18 @@
 
 
 def kernel(
-    shape, w_ref, h_ref, conn_ref, im_ref, cnt_ref, filt_ref, marg_ref,
-    st, thi, tlo, ahi, alo, mext, imx, vext, ys, us_f, us, ur, rb, lb, pacc, px,
-    es, er, zs, zr,
-    s_w, r_w, s_im, r_im, s_u, r_u, s_r, r_r, s_l, r_l, s_p, r_p, s_e, r_e, s_z, r_z,
+    shape, w_hbm, h_hbm, conn_hbm, im_hbm, cnt_ref, filt_ref, marg_ref,
+    h_ref, conn_ref, im_ref, s_in,
+    st, thi, tlo, ahi, alo, mext, imx, vext, ys, us_f, us, ur, rb, lb, pp, px, pb,
+    esa, era, esb, erb, esm, erm, ms, mr, zs, zr,
+    s_w, r_w, s_im, r_im, s_u, r_u, s_r, r_r, s_l, r_l, s_p, r_p, s_ea, r_ea, s_eb, r_eb, s_em, r_em, s_m, r_m, s_z, r_z,
 ):
     nx, ny, nh, nz = shape
-    own, width = w_ref.shape
+    own, width = w_hbm.shape
     cells, npc, _ = h_ref.shape
     ghost = own // 4
     ext = own + 2 * ghost
     block = 2 * ghost
-    hh = nh // 2
     out_rows = width // 4
     domains = ny * nz * 2
 
@@ -62,6 +62,18 @@
             return dev(x, y, at("h", step), zl, c)
         return dev(at("x", step), y, zh, zl, c)
 
+    loads = [
+        pltpu.make_async_copy(w_hbm, vext.at[slice(ghost, ghost + own)], s_in.at[0]),
+        pltpu.make_async_copy(im_hbm, im_ref, s_in.at[1]),
+        pltpu.make_async_copy(conn_hbm, conn_ref, s_in.at[2]),
+        pltpu.make_async_copy(h_hbm, h_ref, s_in.at[3]),
+    ]
+    for one in loads:
+        one.start()
+
+    toward = 2 * c - 1
+    mirror = dev(x, y, at("h", toward), zl, 1 - c)
+
     barrier = pltpu.get_barrier_semaphore()
 
     def greet(where):
@@ -71,8 +83,8 @@
     right = (lax.rem(d + 1, domains), b)
     greet(left)
     greet(right)
-    greet(beside("h", 1))
-    greet(beside("h", -1))
+    greet(beside("h", toward))
+    greet(mirror)
     if nx > 1:
         greet(beside("x", 1))
         greet(beside("x", -1))
@@ -81,10 +93,32 @@
     for yy in range(ny):
         pl.when(jnp.logical_not((x == y) & (y == yy)))(
             functools.partial(greet, dev(y, yy, zh, zl, c)))
-    half = lax.div(zl, nz // 2)
+    for yy in range(ny):
+        pl.when(y != yy)(functools.partial(greet, dev(x, yy, zh, zl, c)))
+    ahead = lax.rem(lax.div(zl, 2) + nh - zh, nh)
+    half = jnp.where((ahead == 1) | (ahead == 2), 1, 0)
     for lz in range(nz):
         pl.when(jnp.logical_not((zl == lz) & (c == half)))(
             functools.partial(greet, dev(x, y, zh, lz, half)))
+
+    loads[0].wait()
+    loads[1].wait()
+    as_int = lambda flag: flag.astype(jnp.int32)
+    total = (2 + 2 + (2 if nx > 1 else 0) + 1 + (nx - as_int(x == y)) + (ny - 1)
+             + (nz - as_int(half == c)))
+    pl.semaphore_wait(barrier, total)
+
+    first = []
+    for side, where in ((0, left), (1, right)):
+        other = 1 - side
+        rows = slice(ghost, 2 * ghost) if side == 0 else slice(own, own + ghost)
+        land = slice(own + ghost, ext) if side == 0 else slice(0, ghost)
+        first.append(copy(im_ref, imx.at[other], s_im.at[side], r_im.at[other], where))
+        first.append(copy(vext.at[rows], vext.at[land], s_w.at[side], r_w.at[other], where))
+    for one in first:
+        one.start()
+    for one in loads[2:]:
+        one.wait()
 
     for cell in range(cells):
         live = cell < cnt_ref[0]
@@ -132,24 +166,8 @@
 
     for i in range(4):
         mext[ghost * (i + 1):ghost * (i + 2), :] = spread(im_ref[i:i + 1, :])
-    vext[ghost:ghost + own, :] = w_ref[...]
-
-    as_int = lambda flag: flag.astype(jnp.int32)
-    total = (2 + 2 + (2 if nx > 1 else 0) + 1 + (nx - as_int(x == y))
-             + (nz - as_int(half == c)))
-    pl.semaphore_wait(barrier, total)
-
-    first = []
-    for side, where in ((0, left), (1, right)):
-        other = 1 - side
-        rows = slice(0, ghost) if side == 0 else slice(own - ghost, own)
-        land = slice(own + ghost, ext) if side == 0 else slice(0, ghost)
-        first.append(copy(im_ref, imx.at[other], s_im.at[side], r_im.at[other], where))
-        first.append(copy(w_ref.at[rows], vext.at[land], s_w.at[side], r_w.at[other], where))
     for one in first:
-        one.start()
-    for one in first:
-        one.wait_recv()
+        one.wait()
     mext[0:ghost, :] = spread(imx[0, 3:4, :])
     mext[own + ghost:ext, :] = spread(imx[1, 0:1, :])
     ys[0] = vext[...].astype(jnp.float32)
@@ -198,39 +216,33 @@
         rb[x, rows, :] = value
         filt_ref[rows, :] = value
 
-    def piece_rows(core, p):
-        if p == 0:
-            return pl.ds(pl.multiple_of((1 - core) * ghost, ghost), 3 * ghost)
-        return pl.ds(pl.multiple_of(core * 3 * ghost, ghost), ghost)
-
-    bufs = {"h": (lb, s_l, r_l), "x": (rb, s_r, r_r)}
-    toward = 2 * c - 1
-
-    def block_send(axis, i, p):
-        buf, send, recv = bufs[axis]
-        step = (1, -1, -toward)[i]
-        slot = ring[axis][0] if i < 2 else at(axis, toward)
-        ref = buf.at[slot, piece_rows(c, p)]
-        return copy(ref, ref, send.at[i, p], recv.at[i, p], beside(axis, step))
-
-    def block_recv(axis, i, p):
-        buf, send, recv = bufs[axis]
-        slot = at(axis, (-1, 1, 2)[i])
-        step = (-1, 1, toward)[i]
-        ref = buf.at[slot, piece_rows(c, p)]
-        return copy(ref, ref, send.at[i, p], recv.at[i, p], beside(axis, step))
-
-    axes = ("h", "x") if nx > 1 else ("h",)
+    def piece_rows(p):
+        off, size = (((1 - c) * ghost, 3 * ghost), (c * 3 * ghost, ghost))[p]
+        return pl.ds(pl.multiple_of(off, ghost), size)
+
+    def x_send(i, p):
+        slot = x if i < 2 else at("x", toward)
+        ref = rb.at[slot, piece_rows(p)]
+        return copy(ref, ref, s_r.at[i, p], r_r.at[i, p], beside("x", (1, -1, -toward)[i]))
+
+    def x_recv(i, p):
+        ref = rb.at[at("x", (-1, 1, 2)[i]), piece_rows(p)]
+        return copy(ref, ref, s_r.at[i, p], r_r.at[i, p], beside("x", (-1, 1, toward)[i]))
+
+    def h_send(i, p):
+        slot = zh if i == 0 else at("h", toward)
+        ref = lb.at[slot, piece_rows(p)]
+        return copy(ref, ref, s_l.at[i, p], r_l.at[i, p], beside("h", -toward))
+
+    def h_recv(i, p):
+        ref = lb.at[at("h", toward if i == 0 else 2), piece_rows(p)]
+        return copy(ref, ref, s_l.at[i, p], r_l.at[i, p], beside("h", toward))
 
     def send_piece(p):
-        for axis in axes:
-            for i in range(2):
-                block_send(axis, i, p).start()
-
-    def pass_on(axis, p):
-        for i in range(2):
-            block_recv(axis, i, p).wait_recv()
-        block_send(axis, 2, p).start()
+        h_send(0, p).start()
+        if nx > 1:
+            x_send(0, p).start()
+            x_send(1, p).start()
 
     for k in range(DEGREE):
         last = k == DEGREE - 1
@@ -269,65 +281,57 @@
                 vext[rows, :] = value
 
     for p in range(2):
-        for axis in reversed(axes):
-            pass_on(axis, p)
+        if nx > 1:
+            for i in range(2):
+                x_recv(i, p).wait_recv()
+            x_send(2, p).start()
+        h_recv(0, p).wait_recv()
+        h_send(1, p).start()
     if nx > 1:
         for p in range(2):
-            block_recv("x", 2, p).wait_recv()
+            x_recv(2, p).wait_recv()
+
+    def over_nodes(left_op, right_op):
+        return lax.dot_general(left_op, right_op, (((0,), (0,)), ((), ())),
+                               preferred_element_type=jnp.float32)
+
     right_op = jnp.concatenate([rb[xx] for xx in range(nx)], axis=1)
-
-    def p_rows(o):
-        return pl.ds(pl.multiple_of(o * width, width), width)
-
-    def p_send(o):
-        h = lax.rem(o, hh)
-        return copy(pacc.at[p_rows(o)], px.at[h], s_p.at[h], r_p.at[h], partner)
-
-    def p_recv(h):
-        return copy(px.at[h], px.at[h], s_p.at[h], r_p.at[h], partner)
-
-    for step in (0, -1, 1, 2):
-        o = at("h", step)
-        if step == 2:
-            for p in range(2):
-                block_recv("h", 2, p).wait_recv()
-        pacc[p_rows(o), :] = lax.dot_general(
-            lb[o], right_op, (((0,), (0,)), ((), ())), preferred_element_type=jnp.float32)
-        pl.when(lax.div(o, hh) != c)(lambda o=o: p_send(o).start())
-    for h in range(hh):
-        p_recv(h).wait_recv()
-
-    def e_send(xx):
-        return copy(es.at[xx], er.at[y], s_e.at[xx], r_e.at[y], dev(xx, x, zh, zl, c))
-
-    def e_recv(yy):
-        return copy(er.at[yy], er.at[yy], s_e.at[yy], r_e.at[yy], dev(y, yy, zh, zl, c))
-
-    sums = [pacc[p_rows(c * hh + h), :] + px[h] for h in range(hh)]
-    for xx in range(nx):
-        cols = slice(xx * width, (xx + 1) * width)
-        value = jnp.concatenate([one[:, cols] for one in sums], axis=0).astype(es.dtype)
-        away = jnp.logical_not((x == xx) & (x == y))
-
-        @pl.when(away)
-        def _(xx=xx, value=value):
-            es[xx] = value
-            e_send(xx).start()
-
-        @pl.when(jnp.logical_not(away))
-        def _(value=value):
-            er[y] = value
-    acc = None
-    for yy in range(ny):
-        pl.when(jnp.logical_not((x == y) & (y == yy)))(lambda yy=yy: e_recv(yy).wait_recv())
-        term = er[yy].astype(jnp.float32)
-        acc = term if acc is None else acc + term
-    zs[...] = acc.astype(zs.dtype)
-
-    targets = 2 * (nz // 2)
+    p_copy = copy(pp.at[1], px, s_p.at[0], r_p.at[0], partner)
+
+    def e_copy(src, dst, send, recv, xx):
+        return copy(src.at[xx], dst.at[y], send.at[xx], recv.at[y], dev(xx, x, zh, zl, c))
+
+    def e_away(xx):
+        return jnp.logical_not((x == xx) & (x == y))
+
+    def spread_out(value_of, src, dst, send, recv):
+        for xx in range(nx):
+            value = value_of(slice(xx * width, (xx + 1) * width)).astype(src.dtype)
+
+            @pl.when(e_away(xx))
+            def _(xx=xx, value=value):
+                src[xx] = value
+                e_copy(src, dst, send, recv, xx).start()
+
+            @pl.when(jnp.logical_not(e_away(xx)))
+            def _(value=value):
+                dst[y] = value
+
+    def collected(dst, send, recv):
+        acc = None
+        for yy in range(ny):
+            here = copy(dst.at[yy], dst.at[yy], send.at[yy], recv.at[yy], dev(y, yy, zh, zl, c))
+            pl.when(jnp.logical_not((x == y) & (y == yy)))(here.wait_recv)
+            term = dst[yy].astype(jnp.float32)
+            acc = term if acc is None else acc + term
+        return acc
+
+    def em_send(xx):
+        return copy(esm.at[xx], erm.at[y], s_em.at[xx], r_em.at[y], dev(x, xx, zh, zl, c))
 
     def z_target(j):
-        return c * (nz // 2) + j // 2, j % 2
+        kept = at("h", toward) if j >= 4 else jnp.where(c == 0, zh, at("h", 2))
+        return kept * 2 + (j // 2) % 2, j % 2
 
     def z_away(j):
         lz, core = z_target(j)
@@ -341,12 +345,53 @@
     def z_recv(lz):
         return copy(zr.at[lz], zr.at[lz], s_z.at[lz], r_z.at[lz], dev(x, y, zh, lz, half))
 
-    for j in range(targets):
-        pl.when(z_away(j))(lambda j=j: z_send(j).start())
-
-        @pl.when(jnp.logical_not(z_away(j)))
-        def _(j=j):
-            zr[zl] = zs[j * out_rows:(j + 1) * out_rows, :]
+    def hand_over(which, value):
+        zs[which * width:(which + 1) * width, :] = value.astype(zs.dtype)
+        for j in range(4 * which, 4 * which + 4):
+            pl.when(z_away(j))(lambda j=j: z_send(j).start())
+
+            @pl.when(jnp.logical_not(z_away(j)))
+            def _(j=j):
+                zr[zl] = zs[j * out_rows:(j + 1) * out_rows, :]
+
+    side = lb[at("h", toward)]
+    for xx in range(nx):
+        value = over_nodes(rb[xx], side).astype(esm.dtype)
+
+        @pl.when(y != xx)
+        def _(xx=xx, value=value):
+            esm[xx] = value
+            em_send(xx).start()
+
+        @pl.when(y == xx)
+        def _(value=value):
+            erm[y] = value
+    pb[...] = over_nodes(side, right_op)
+    spread_out(lambda cols: pb[:, cols], esb, erb, s_eb, r_eb)
+    pp[c] = over_nodes(lb[zh], right_op)
+    pl.when(c == 1)(p_copy.start)
+
+    acc = None
+    for yy in range(ny):
+        here = copy(erm.at[yy], erm.at[yy], s_em.at[yy], r_em.at[yy], dev(x, yy, zh, zl, c))
+        pl.when(y != yy)(here.wait_recv)
+        term = erm[yy].astype(jnp.float32)
+        acc = term if acc is None else acc + term
+    ms[...] = acc.astype(ms.dtype)
+    m_copy = copy(ms, mr, s_m.at[0], r_m.at[0], mirror)
+    m_copy.start()
+    kept = collected(erb, s_eb, r_eb)
+
+    for p in range(2):
+        h_recv(1, p).wait_recv()
+    pp[1 - c] = over_nodes(lb[at("h", 2)], right_op)
+    pl.when(c == 0)(p_copy.start)
+    p_copy.wait_recv()
+    spread_out(lambda cols: pp[0, :, cols] + px[:, cols], esa, era, s_ea, r_ea)
+    m_copy.wait_recv()
+    hand_over(1, kept + mr[...].astype(jnp.float32))
+    hand_over(0, collected(era, s_ea, r_ea))
+
     acc = None
     for lz in range(nz):
         pl.when(jnp.logical_not((zl == lz) & (c == half)))(lambda lz=lz: z_recv(lz).wait_recv())
@@ -354,20 +399,23 @@
         acc = term if acc is None else acc + term
     marg_ref[...] = acc * (1.0 / float(own * domains) ** 0.5)
 
-    for one in first:
-        one.wait_send()
     for k in range(DEGREE):
         for which in range(2):
             u_send(k, which).wait_send()
     for p in range(2):
-        for axis in axes:
-            for i in range(3):
-                block_send(axis, i, p).wait_send()
-    for h in range(hh):
-        p_send((1 - c) * hh + h).wait_send()
+        for i in range(2):
+            h_send(i, p).wait_send()
+        for i in range(3 if nx > 1 else 0):
+            x_send(i, p).wait_send()
+    p_copy.wait_send()
+    m_copy.wait_send()
     for xx in range(nx):
-        pl.when(jnp.logical_not((x == xx) & (x == y)))(lambda xx=xx: e_send(xx).wait_send())
-    for j in range(targets):
+        @pl.when(e_away(xx))
+        def _(xx=xx):
+            e_copy(esa, era, s_ea, r_ea, xx).wait_send()
+            e_copy(esb, erb, s_eb, r_eb, xx).wait_send()
+        pl.when(y != xx)(lambda xx=xx: em_send(xx).wait_send())
+    for j in range(8):
         pl.when(z_away(j))(lambda j=j: z_send(j).wait_send())
 
 
@@ -378,18 +426,22 @@
     ghost = own // 4
     ext = own + 2 * ghost
     block = 2 * ghost
-    hh = nh // 2
     out_rows = width // 4
     bf, f32 = jnp.bfloat16, jnp.float32
-    sent = f32
+    sent = bf
     dma = pltpu.SemaphoreType.DMA
     vm = pl.BlockSpec(memory_space=pltpu.VMEM)
+    hbm = pl.BlockSpec(memory_space=pl.ANY)
     filtered, rows = pl.pallas_call(
         functools.partial(kernel, shape),
         out_shape=(jax.ShapeDtypeStruct((own, width), bf), jax.ShapeDtypeStruct((out_rows, width), f32)),
-        in_specs=[vm, vm, vm, vm, pl.BlockSpec(memory_space=pltpu.SMEM)],
+        in_specs=[hbm, hbm, hbm, hbm, pl.BlockSpec(memory_space=pltpu.SMEM)],
         out_specs=(vm, vm),
         scratch_shapes=[
+            pltpu.VMEM((cells, npc, npc), bf),
+            pltpu.VMEM((cells, npc), jnp.int32),
+            pltpu.VMEM((4, ghost), f32),
+            dma((4,)),
             pltpu.VMEM((ext, cells * npc), bf),
             pltpu.VMEM((cells * npc, ext), bf),
             pltpu.VMEM((cells * npc, ext), bf),
@@ -404,21 +456,29 @@
             pltpu.VMEM((DEGREE, 2, block, width), sent),
             pltpu.VMEM((nx, own, width), bf),
             pltpu.VMEM((nh, own, width), bf),
-            pltpu.VMEM((nh * width, nx * width), f32),
-            pltpu.VMEM((hh, width, nx * width), f32),
-            pltpu.VMEM((nx, hh * width, width), bf),
-            pltpu.VMEM((ny, hh * width, width), bf),
-            pltpu.VMEM((hh * width, width), bf),
+            pltpu.VMEM((2, width, nx * width), f32),
+            pltpu.VMEM((width, nx * width), f32),
+            pltpu.VMEM((width, nx * width), f32),
+            pltpu.VMEM((nx, width, width), bf),
+            pltpu.VMEM((ny, width, width), bf),
+            pltpu.VMEM((nx, width, width), bf),
+            pltpu.VMEM((ny, width, width), bf),
+            pltpu.VMEM((nx, width, width), bf),
+            pltpu.VMEM((ny, width, width), bf),
+            pltpu.VMEM((width, width), bf),
+            pltpu.VMEM((width, width), bf),
+            pltpu.VMEM((2 * width, width), bf),
             pltpu.VMEM((nz, out_rows, width), bf),
             dma((2,)), dma((2,)), dma((2,)), dma((2,)),
             dma((DEGREE, 2)), dma((DEGREE, 2)),
-            dma((3, 2)), dma((3, 2)), dma((3, 2)), dma((3, 2)),
-            dma((hh,)), dma((hh,)),
-            dma((nx,)), dma((ny,)),
-            dma((nz,)), dma((nz,)),
+            dma((3, 2)), dma((3, 2)), dma((2, 2)), dma((2, 2)),
+            dma((1,)), dma((1,)),
+            dma((nx,)), dma((ny,)), dma((nx,)), dma((ny,)), dma((nx,)), dma((ny,)),
+            dma((1,)), dma((1,)),
+            dma((8,)), dma((nz,)),
         ],
         compiler_params=pltpu.CompilerParams(
-            collective_id=0, has_side_effects=True, vmem_limit_bytes=48 * 1024 * 1024),
+            collective_id=0, has_side_effects=True, vmem_limit_bytes=67043328),
         name="filter_margin",
     )(wavefunctions, cell_ham, connectivity, inv_mass.reshape(4, ghost), cell_count)
     return filtered, rows.T

time: 117 us -> 105 us (0.90)
  the two profiles are of different devices: /device:TPU:17 before, /device:TPU:1 now
where the time goes in v3:
time: 105 us
  Pallas kernels  101 us (96%)
  local copies, waits for them, and re-layouts  2.18 us (2%)
  between operations  1.29 us (1%)
    pallas_call x1, Pallas kernels, local(): pl.pallas_call(functools.partial(kernel, shape), out_shape=(jax.ShapeDtyp...  101 us
    unnamed x4, local copies, waits for them, and re-layouts  2.18 us

profile of v3, /device:TPU:1, one launch (start us, length us, event | category | flops | bytes accessed | tf_op | source)
XLA Modules:
  0.0 104.8 jit_solution(153484186277205206)
XLA Ops:
  1.3 101.3 %filter_margin.1 = (bf16[512,128]{1,0:T(8,128)(2,1)}, f32[32,128]{1,0:T(8,128)}) custom-call(bf16[512,128]{1,0:T(8,128)(2,1)} %w_hbm.1, bf16[2,512,512]{2,1,0:T(8,128)(2,1)} %h_hbm.1, s32[2,512]{1,0:T(2,128)} %conn_hbm.1, f32[4,128]{1,0:T(4,128)} %bitcast.3, s32[1]{0:T(128)S(6)} %copy.9.cnt_ref), custom_call_target="tpu_custom_call" | custom-call | tf_op jit(solution)/shard_map/filter_margin/pallas_call | solution.py:435
  102.6 0.0 copy-start
  102.6 1.6 %copy.10 = bf16[512,128]{1,0:T(8,128)(2,1)} copy(bf16[512,128]{1,0:T(8,128)(2,1)} %get-tuple-element.8) | data formatting | bytes 262144
  104.2 0.0 copy-done
  104.2 0.6 copy.11
Async XLA Ops:
  102.6 1.6 %copy-start = (f32[32,128]{1,0:T(8,128)S(1)}, f32[32,128]{1,0:T(8,128)}, u32[]{:S(2)}) copy-start(f32[32,128]{1,0:T(8,128)} %get-tuple-element.5) | copy-start | bytes 49156

commit v4 on v3

--- a/solution.py
+++ b/solution.py
@@ -11,6 +11,7 @@
 CENTER = 0.5
 HALFWIDTH = 3.0
 NX, NY, NH, NZ = 4, 4, 4, 8
+PACED = 2
 MESH = pl.DeviceIdType.MESH
 
 
@@ -21,7 +22,7 @@
 def kernel(
     shape, w_hbm, h_hbm, conn_hbm, im_hbm, cnt_ref, filt_ref, marg_ref,
     h_ref, conn_ref, im_ref, s_in,
-    st, thi, tlo, ahi, alo, mext, imx, vext, ys, us_f, us, ur, rb, lb, pp, px, pb,
+    st, thi, tlo, ahi, alo, mext, imx, vext, ys, us_f, upart, us, ur, rb, lb, pp, px, pb,
     esa, era, esb, erb, esm, erm, ms, mr, zs, zr,
     s_w, r_w, s_im, r_im, s_u, r_u, s_r, r_r, s_l, r_l, s_p, r_p, s_ea, r_ea, s_eb, r_eb, s_em, r_em, s_m, r_m, s_z, r_z,
 ):
@@ -101,22 +102,6 @@
         pl.when(jnp.logical_not((zl == lz) & (c == half)))(
             functools.partial(greet, dev(x, y, zh, lz, half)))
 
-    loads[0].wait()
-    loads[1].wait()
-    as_int = lambda flag: flag.astype(jnp.int32)
-    total = (2 + 2 + (2 if nx > 1 else 0) + 1 + (nx - as_int(x == y)) + (ny - 1)
-             + (nz - as_int(half == c)))
-    pl.semaphore_wait(barrier, total)
-
-    first = []
-    for side, where in ((0, left), (1, right)):
-        other = 1 - side
-        rows = slice(ghost, 2 * ghost) if side == 0 else slice(own, own + ghost)
-        land = slice(own + ghost, ext) if side == 0 else slice(0, ghost)
-        first.append(copy(im_ref, imx.at[other], s_im.at[side], r_im.at[other], where))
-        first.append(copy(vext.at[rows], vext.at[land], s_w.at[side], r_w.at[other], where))
-    for one in first:
-        one.start()
     for one in loads[2:]:
         one.wait()
 
@@ -144,6 +129,22 @@
             return carry
         lax.fori_loop(0, (npc // rt) * (ext // ct), gather_cols, 0)
 
+    loads[0].wait()
+    loads[1].wait()
+    as_int = lambda flag: flag.astype(jnp.int32)
+    total = (2 + 2 + (2 if nx > 1 else 0) + 1 + (nx - as_int(x == y)) + (ny - 1)
+             + (nz - as_int(half == c)))
+    pl.semaphore_wait(barrier, total)
+
+    first = []
+    for side, where in ((0, left), (1, right)):
+        other = 1 - side
+        rows = slice(ghost, 2 * ghost) if side == 0 else slice(own, own + ghost)
+        land = slice(own + ghost, ext) if side == 0 else slice(0, ghost)
+        first.append(copy(im_ref, imx.at[other], s_im.at[side], r_im.at[other], where))
+        first.append(copy(vext.at[rows], vext.at[land], s_w.at[side], r_w.at[other], where))
+    for one in first:
+        one.start()
     art = tile_of(ext, 256)
 
     def scatter_rows(i, carry):
@@ -229,64 +230,92 @@
         ref = rb.at[at("x", (-1, 1, 2)[i]), piece_rows(p)]
         return copy(ref, ref, s_r.at[i, p], r_r.at[i, p], beside("x", (-1, 1, toward)[i]))
 
-    def h_send(i, p):
+    def chunk_rows(q):
+        off = (q + 1 - c) * ghost if q < 3 else c * 3 * ghost
+        return pl.ds(pl.multiple_of(off, ghost), ghost)
+
+    def h_send(i, q):
         slot = zh if i == 0 else at("h", toward)
-        ref = lb.at[slot, piece_rows(p)]
-        return copy(ref, ref, s_l.at[i, p], r_l.at[i, p], beside("h", -toward))
-
-    def h_recv(i, p):
-        ref = lb.at[at("h", toward if i == 0 else 2), piece_rows(p)]
-        return copy(ref, ref, s_l.at[i, p], r_l.at[i, p], beside("h", toward))
+        ref = lb.at[slot, chunk_rows(q)]
+        return copy(ref, ref, s_l.at[i, q], r_l.at[i, q], beside("h", -toward))
+
+    def h_recv(i, q):
+        ref = lb.at[at("h", toward if i == 0 else 2), chunk_rows(q)]
+        return copy(ref, ref, s_l.at[i, q], r_l.at[i, q], beside("h", toward))
+
+    paced = (zl >= PACED) & (zl < nz - PACED)
 
     def send_piece(p):
-        h_send(0, p).start()
+        if p == 0:
+            h_send(0, 0).start()
+            h_send(0, 1).start()
+            pl.when(jnp.logical_not(paced))(lambda: h_send(0, 2).start())
+        else:
+            pl.when(jnp.logical_not(paced))(lambda: h_send(0, 3).start())
         if nx > 1:
             x_send(0, p).start()
             x_send(1, p).start()
 
+    far_rows = pl.ds(pl.multiple_of(c * own, block), block)
+    near_rows = pl.ds(pl.multiple_of((1 - c) * own, block), block)
+    rest_rows = pl.ds(pl.multiple_of((1 - c) * block, block), own)
+    mid = slice(block, own)
+
+    def part_product(rows, cols):
+        v = vext[cols, :]
+        return (jnp.dot(ahi[rows, cols], v, preferred_element_type=jnp.float32)
+                + jnp.dot(alo[rows, cols], v, preferred_element_type=jnp.float32))
+
+    def emit(k, which, rows, u):
+        us_f[rows, :] = u
+        us[k, side_of(which)] = u.astype(us.dtype)
+        u_send(k, which).start()
+
+    def settle(k, which, rows):
+        s = side_of(which)
+        u_recv(k, which).wait_recv()
+        if k < DEGREE - 1:
+            return advance(k, rows, us_f[rows, :] + ur[k, s].astype(jnp.float32))
+        inner = pl.multiple_of((1 - s) * ghost, ghost)
+        rows = pl.ds(pl.multiple_of(s * own + inner, ghost), ghost)
+        new = advance(
+            k, rows, us_f[rows, :] + ur[k, s, pl.ds(inner, ghost), :].astype(jnp.float32))
+        place(pl.multiple_of(s * 3 * ghost, ghost), ghost, new)
+        send_piece(1 - which)
+        return None
+
     for k in range(DEGREE):
         last = k == DEGREE - 1
-        offs = []
-        for which in range(2):
-            s = side_of(which)
-            off = pl.multiple_of(s * own, block)
-            offs.append((s, off))
-            u = product(pl.ds(off, block))
-            us_f[pl.ds(off, block), :] = u
-            us[k, s] = u.astype(us.dtype)
-            u_send(k, which).start()
-        mid = slice(block, own)
+        if k == 0:
+            emit(k, 0, far_rows, product(far_rows))
+        else:
+            emit(k, 0, far_rows, upart[...] + part_product(far_rows, far_rows))
+        emit(k, 1, near_rows, product(near_rows))
         mid_new = advance(k, mid, product(mid))
         if last:
             place(ghost, own - block, mid_new)
-        fresh = []
-        for which in (1, 0):
-            s, off = offs[which]
-            u_recv(k, which).wait_recv()
-            if not last:
-                rows = pl.ds(off, block)
-                fresh.append((rows, advance(
-                    k, rows, us_f[rows, :] + ur[k, s].astype(jnp.float32))))
-            else:
-                inner = pl.multiple_of((1 - s) * ghost, ghost)
-                rows = pl.ds(pl.multiple_of(off + inner, ghost), ghost)
-                new = advance(
-                    k, rows,
-                    us_f[rows, :] + ur[k, s, pl.ds(inner, ghost), :].astype(jnp.float32))
-                place(pl.multiple_of(s * 3 * ghost, ghost), ghost, new)
-                send_piece(1 - which)
-        if not last:
+            settle(k, 1, near_rows)
+            settle(k, 0, far_rows)
+        else:
+            near_new = settle(k, 1, near_rows)
             vext[mid, :] = mid_new
-            for rows, value in fresh:
-                vext[rows, :] = value
+            vext[near_rows, :] = near_new
+            upart[...] = part_product(far_rows, rest_rows)
+            vext[far_rows, :] = settle(k, 0, far_rows)
 
     for p in range(2):
         if nx > 1:
             for i in range(2):
                 x_recv(i, p).wait_recv()
             x_send(2, p).start()
-        h_recv(0, p).wait_recv()
-        h_send(1, p).start()
+        for q in ((0, 1, 2), (3,))[p]:
+            h_recv(0, q).wait_recv()
+            if q == 1:
+                @pl.when(paced)
+                def _():
+                    h_send(0, 2).start()
+                    h_send(0, 3).start()
+            h_send(1, q).start()
     if nx > 1:
         for p in range(2):
             x_recv(2, p).wait_recv()
@@ -382,8 +411,8 @@
     m_copy.start()
     kept = collected(erb, s_eb, r_eb)
 
-    for p in range(2):
-        h_recv(1, p).wait_recv()
+    for q in range(4):
+        h_recv(1, q).wait_recv()
     pp[1 - c] = over_nodes(lb[at("h", 2)], right_op)
     pl.when(c == 0)(p_copy.start)
     p_copy.wait_recv()
@@ -403,8 +432,9 @@
         for which in range(2):
             u_send(k, which).wait_send()
     for p in range(2):
-        for i in range(2):
-            h_send(i, p).wait_send()
+        for q in range(4 if p == 0 else 0):
+            h_send(0, q).wait_send()
+            h_send(1, q).wait_send()
         for i in range(3 if nx > 1 else 0):
             x_send(i, p).wait_send()
     p_copy.wait_send()
@@ -452,6 +482,7 @@
             pltpu.VMEM((ext, width), bf),
             pltpu.VMEM((2, ext, width), f32),
             pltpu.VMEM((ext, width), f32),
+            pltpu.VMEM((block, width), f32),
             pltpu.VMEM((DEGREE, 2, block, width), sent),
             pltpu.VMEM((DEGREE, 2, block, width), sent),
             pltpu.VMEM((nx, own, width), bf),
@@ -471,7 +502,7 @@
             pltpu.VMEM((nz, out_rows, width), bf),
             dma((2,)), dma((2,)), dma((2,)), dma((2,)),
             dma((DEGREE, 2)), dma((DEGREE, 2)),
-            dma((3, 2)), dma((3, 2)), dma((2, 2)), dma((2, 2)),
+            dma((3, 2)), dma((3, 2)), dma((2, 4)), dma((2, 4)),
             dma((1,)), dma((1,)),
             dma((nx,)), dma((ny,)), dma((nx,)), dma((ny,)), dma((nx,)), dma((ny,)),
             dma((1,)), dma((1,)),

time: 105 us -> 98 us (0.933)
  Pallas kernels: 101 us -> 94.3 us
    pallas_call x1, Pallas kernels: 101 us -> 94.3 us  [local(): pl.pallas_call(functools.partial(kernel, shape), out_shape=(jax.ShapeDtyp...]
where the time goes in v4:
time: 98 us; the launch traced here: 97.8 us
  Pallas kernels  94.3 us (96%)
  local copies, waits for them, and re-layouts  2.18 us (2%)
  between operations  1.29 us (1%)
    pallas_call x1, Pallas kernels, local(): pl.pallas_call(functools.partial(kernel, shape), out_shape=(jax.ShapeDtyp...  94.3 us
    unnamed x4, local copies, waits for them, and re-layouts  2.18 us

profile of v4, /device:TPU:1, one launch (start us, length us, event | category | flops | bytes accessed | tf_op | source)
XLA Modules:
  0.0 97.8 jit_solution(3478182015232489834)
XLA Ops:
  1.3 94.3 %filter_margin.1 = (bf16[512,128]{1,0:T(8,128)(2,1)}, f32[32,128]{1,0:T(8,128)}) custom-call(bf16[512,128]{1,0:T(8,128)(2,1)} %w_hbm.1, bf16[2,512,512]{2,1,0:T(8,128)(2,1)} %h_hbm.1, s32[2,512]{1,0:T(2,128)} %conn_hbm.1, f32[4,128]{1,0:T(4,128)} %bitcast.3, s32[1]{0:T(128)S(6)} %copy.9.cnt_ref), custom_call_target="tpu_custom_call" | custom-call | tf_op jit(solution)/shard_map/filter_margin/pallas_call | solution.py:465
  95.6 0.0 copy-start
  95.6 1.6 %copy.10 = bf16[512,128]{1,0:T(8,128)(2,1)} copy(bf16[512,128]{1,0:T(8,128)(2,1)} %get-tuple-element.8) | data formatting | bytes 262144
  97.2 0.0 copy-done
  97.2 0.6 copy.11
Async XLA Ops:
  95.6 1.6 %copy-start = (f32[32,128]{1,0:T(8,128)S(1)}, f32[32,128]{1,0:T(8,128)}, u32[]{:S(2)}) copy-start(f32[32,128]{1,0:T(8,128)} %get-tuple-element.5) | copy-start | bytes 49156

commit v5 on v4

--- a/solution.py
+++ b/solution.py
@@ -128,23 +128,25 @@
             tlo[pl.ds(cell * npc + r, rt), pl.ds(e, ct)] = (t - hi.astype(jnp.float32)).astype(jnp.bfloat16)
             return carry
         lax.fori_loop(0, (npc // rt) * (ext // ct), gather_cols, 0)
-
-    loads[0].wait()
-    loads[1].wait()
-    as_int = lambda flag: flag.astype(jnp.int32)
-    total = (2 + 2 + (2 if nx > 1 else 0) + 1 + (nx - as_int(x == y)) + (ny - 1)
-             + (nz - as_int(half == c)))
-    pl.semaphore_wait(barrier, total)
-
-    first = []
-    for side, where in ((0, left), (1, right)):
-        other = 1 - side
-        rows = slice(ghost, 2 * ghost) if side == 0 else slice(own, own + ghost)
-        land = slice(own + ghost, ext) if side == 0 else slice(0, ghost)
-        first.append(copy(im_ref, imx.at[other], s_im.at[side], r_im.at[other], where))
-        first.append(copy(vext.at[rows], vext.at[land], s_w.at[side], r_w.at[other], where))
-    for one in first:
-        one.start()
+        if cell > 0:
+            continue
+        loads[0].wait()
+        loads[1].wait()
+        as_int = lambda flag: flag.astype(jnp.int32)
+        total = (2 + 2 + (2 if nx > 1 else 0) + 1 + (nx - as_int(x == y)) + (ny - 1)
+                 + (nz - as_int(half == c)))
+        pl.semaphore_wait(barrier, total)
+
+        first = []
+        for side, where in ((0, left), (1, right)):
+            other = 1 - side
+            rows = slice(ghost, 2 * ghost) if side == 0 else slice(own, own + ghost)
+            land = slice(own + ghost, ext) if side == 0 else slice(0, ghost)
+            first.append(copy(im_ref, imx.at[other], s_im.at[side], r_im.at[other], where))
+            first.append(copy(vext.at[rows], vext.at[land], s_w.at[side], r_w.at[other], where))
+        for one in first:
+            one.start()
+
     art = tile_of(ext, 256)
 
     def scatter_rows(i, carry):

time: 98 us -> 100 us (1.020)
  Pallas kernels: 94.3 us -> 96 us
    pallas_call x1, Pallas kernels: 94.3 us -> 96 us  [local(): pl.pallas_call(functools.partial(kernel, shape), out_shape=(jax.ShapeDtyp...]
where the time goes in v5:
time: 100 us; the launch traced here: 99.5 us
  Pallas kernels  96 us (96%)
  local copies, waits for them, and re-layouts  2.18 us (2%)
  between operations  1.29 us (1%)
    pallas_call x1, Pallas kernels, local(): pl.pallas_call(functools.partial(kernel, shape), out_shape=(jax.ShapeDtyp...  96 us
    unnamed x4, local copies, waits for them, and re-layouts  2.18 us

profile of v5, /device:TPU:1, one launch (start us, length us, event | category | flops | bytes accessed | tf_op | source)
XLA Modules:
  0.0 99.5 jit_solution(215271416156706110)
XLA Ops:
  1.3 96.0 %filter_margin.1 = (bf16[512,128]{1,0:T(8,128)(2,1)}, f32[32,128]{1,0:T(8,128)}) custom-call(bf16[512,128]{1,0:T(8,128)(2,1)} %w_hbm.1, bf16[2,512,512]{2,1,0:T(8,128)(2,1)} %h_hbm.1, s32[2,512]{1,0:T(2,128)} %conn_hbm.1, f32[4,128]{1,0:T(4,128)} %bitcast.3, s32[1]{0:T(128)S(6)} %copy.9.cnt_ref), custom_call_target="tpu_custom_call" | custom-call | tf_op jit(solution)/shard_map/filter_margin/pallas_call | solution.py:467
  97.3 0.0 copy-start
  97.3 1.6 %copy.10 = bf16[512,128]{1,0:T(8,128)(2,1)} copy(bf16[512,128]{1,0:T(8,128)(2,1)} %get-tuple-element.8) | data formatting | bytes 262144
  98.9 0.0 copy-done
  98.9 0.6 copy.11
Async XLA Ops:
  97.3 1.6 %copy-start = (f32[32,128]{1,0:T(8,128)S(1)}, f32[32,128]{1,0:T(8,128)}, u32[]{:S(2)}) copy-start(f32[32,128]{1,0:T(8,128)} %get-tuple-element.5) | copy-start | bytes 49156
